TPU v7x, 32 devices: a whole 2x2x4 slice. The times are simulated.
32 devices in a mesh: dp: 2 (over x), row: 4 (over y, core), col: 4 (over z).
Axes of the slice: x: 2, y: 2, z: 4, core: 2. Of those that a mesh axis runs over, the one named last changes fastest.
Arguments:
- inputs: bfloat16 [12288, 4, 384], P(('dp', 'row'), 'col'), may hold values from -6 to 6
- segment_ids: int32 [24576], P(('dp', 'row')), may hold values from 0 to 95, never falling along the last dimension, each value on 1 to 800 neighbouring positions
- keep_mask: int32 [24576], P(('dp', 'row')), may hold values from 0 to 1, as said below
- query_weight: bfloat16 [768, 192], P('col', 'row'), may hold values from -0.4375 to 0.4375
- query_bias: float32 [768], P('col'), may hold values from -3 to 3
- key_weight: bfloat16 [768, 192], P('col', 'row'), may hold values from -0.4375 to 0.4375
- value_weight: bfloat16 [768, 192], P('col', 'row'), may hold values from -0.4375 to 0.4375
- value_bias: float32 [768], P('col'), may hold values from -3 to 3
- output_weight: bfloat16 [768, 768], P('col', 'row'), may hold values from -0.875 to 0.875
- output_bias: float32 [768], P('col'), may hold values from -3 to 3
- first_gain: float32 [768], P('col'), may hold values from 0.5 to 1.5
- first_shift: float32 [768], P('col'), may hold values from -3 to 3
- expand_weight: bfloat16 [768, 768], P('col', 'row'), may hold values from -0.4375 to 0.4375
- expand_bias: float32 [3072], P('col'), may hold values from -3 to 3
- reduce_weight: bfloat16 [3072, 192], P('col', 'row'), may hold values from -0.21875 to 0.21875
- reduce_bias: float32 [768], P('col'), may hold values from -3 to 3
- second_gain: float32 [768], P('col'), may hold values from 0.5 to 1.5
- second_shift: float32 [768], P('col'), may hold values from -3 to 3
- cotangent: bfloat16 [12288, 4, 384], P(('dp', 'row'), 'col'), may hold values from -6 to 6
Outputs:
- output: bfloat16 [12288, 4, 384], P(('dp', 'row'), 'col')
- input_grad: float32 [12288, 4, 384], P(('dp', 'row'), 'col')
- query_weight_grad: float32 [768, 192], P('col', 'row')
- query_bias_grad: float32 [768], P('col')
- key_weight_grad: float32 [768, 192], P('col', 'row')
- value_weight_grad: float32 [768, 192], P('col', 'row')
- value_bias_grad: float32 [768], P('col')
- output_weight_grad: float32 [768, 768], P('col', 'row')
- output_bias_grad: float32 [768], P('col')
- first_gain_grad: float32 [768], P('col')
- first_shift_grad: float32 [768], P('col')
- expand_weight_grad: float32 [768, 768], P('col', 'row')
- expand_bias_grad: float32 [3072], P('col')
- reduce_weight_grad: float32 [3072, 192], P('col', 'row')
- reduce_bias_grad: float32 [768], P('col')
- second_gain_grad: float32 [768], P('col')
- second_shift_grad: float32 [768], P('col')
Inputs may be any that keep to these rules, and one draw needn't show every extreme that they name: `segment_ids`: along the tokens the number never falls; each document holds 1 to 800 tokens and one holds exactly 800; a document may run on into the next sequence. `keep_mask`: in each sequence of 1024 tokens the real tokens come first, 512 of them or more.
All inputs are finite; a program needn't handle non-finite values.
Results may differ from a plain program's by a relative error of at most 0.02.
Values may be sent and summed in bfloat16 or wider, within the bound.
A program may use at most 128 MiB of HBM per device.

v0:
```python
import jax
import jax.numpy as jnp
from jax import lax
from jax.sharding import PartitionSpec as P

D = 768
HEAD_DIM = 64
LEN = 1024


EPSILON = 1e-05
NEGATIVE = -1e30
ROOT_HALF = 0.7071067811865476
DENSITY_SCALE = 0.3989422804014327


def as_rows(paired):
    return paired.reshape(paired.shape[0] * 2, paired.shape[2] // 2)


def as_pairs(matrix):
    return matrix.reshape(matrix.shape[0] // 2, 1, matrix.shape[1] * 2)


def forward_product(left, right):
    return jnp.dot(left, right, preferred_element_type=jnp.float32)


def product_transposed(left, right):
    return lax.dot_general(
        left, right, (((1,), (1,)), ((), ())), preferred_element_type=jnp.float32
    )


def product_over_rows(left, right):
    return lax.dot_general(
        left, right, (((0,), (0,)), ((), ())), preferred_element_type=jnp.float32
    )


def norm_forward(summed, norm_gain, norm_shift):
    totals = lax.psum((jnp.sum(summed, axis=1), jnp.sum(summed * summed, axis=1)), "col")
    center = totals[0] / D
    inverse = lax.rsqrt(totals[1] / D - center * center + EPSILON)
    normal = (summed - center[:, None]) * inverse[:, None]
    return (normal * norm_gain + norm_shift, normal, inverse)


def norm_backward(upstream, normal, inverse, norm_gain):
    scaled = upstream * norm_gain
    totals = lax.psum((jnp.sum(scaled, axis=1), jnp.sum(scaled * normal, axis=1)), "col")
    back = inverse[:, None] * (scaled - totals[0][:, None] / D - normal * totals[1][:, None] / D)
    return (back, jnp.sum(upstream * normal, axis=0), jnp.sum(upstream, axis=0))


def allowed_mask(segment_rows, keep_rows, offset, block_rows):
    block_segment = segment_rows[offset : offset + block_rows]
    query_places = offset + jnp.arange(block_rows, dtype=jnp.int32)
    key_places = jnp.arange(segment_rows.shape[0], dtype=jnp.int32)
    same_segment = block_segment[:, None] == segment_rows[None, :]
    return same_segment & (
        (keep_rows[None, :] == 1) | (query_places[:, None] == key_places[None, :])
    )


def block_scores(block_queries, key_rows, allowed):
    raw_scores = jnp.einsum(
        "qhd,khd->hqk", block_queries, key_rows, preferred_element_type=jnp.float32
    ) * HEAD_DIM ** (-0.5)
    return jnp.where(allowed[None], raw_scores, NEGATIVE)


def attention_forward(queries, key_rows, value_rows, segment_ids, keep_mask):
    row_count, channels = queries.shape
    sequences = row_count // LEN
    head_count = channels // HEAD_DIM
    block_rows = min(512, LEN)
    layout = (sequences, LEN, head_count, HEAD_DIM)

    def per_sequence(state_carry, sequence_item):
        seq_queries, seq_keys, seq_values, seq_segment, seq_keep = sequence_item
        outputs = []
        logsums = []
        for block_index in range(LEN // block_rows):
            offset = block_index * block_rows
            allowed = allowed_mask(seq_segment, seq_keep, offset, block_rows)
            scores = block_scores(seq_queries[offset : offset + block_rows], seq_keys, allowed)
            highest = jnp.max(scores, axis=-1, keepdims=True)
            exponent = jnp.exp(scores - highest)
            totals = jnp.sum(exponent, axis=-1, keepdims=True)
            weights = (exponent / totals).astype(jnp.bfloat16)
            outputs.append(
                jnp.einsum("hqk,khd->qhd", weights, seq_values, preferred_element_type=jnp.float32)
            )
            logsums.append((highest + jnp.log(totals))[:, :, 0])
        return (state_carry, (jnp.concatenate(outputs, axis=0), jnp.concatenate(logsums, axis=1)))

    items = (
        queries.reshape(layout),
        key_rows.reshape(layout),
        value_rows.reshape(layout),
        segment_ids.reshape(sequences, LEN),
        keep_mask.reshape(sequences, LEN),
    )
    unused, (context, logsums) = lax.scan(per_sequence, jnp.float32(0), items)
    return (context.reshape(row_count, channels), logsums)


def attention_backward(queries, key_rows, value_rows, segment_ids, keep_mask, logsums, upstream):
    row_count, channels = queries.shape
    sequences = row_count // LEN
    head_count = channels // HEAD_DIM
    block_rows = min(512, LEN)
    layout = (sequences, LEN, head_count, HEAD_DIM)
    score_scale = HEAD_DIM ** (-0.5)

    def per_sequence(state_carry, sequence_item):
        seq_queries, seq_keys, seq_values, seq_segment, seq_keep, seq_logsums, seq_upstream = (
            sequence_item
        )
        key_grad = jnp.zeros(seq_keys.shape, jnp.float32)
        value_grad = jnp.zeros(seq_values.shape, jnp.float32)
        query_grads = []
        for block_index in range(LEN // block_rows):
            offset = block_index * block_rows
            block_queries = seq_queries[offset : offset + block_rows]
            block_upstream = seq_upstream[offset : offset + block_rows]
            allowed = allowed_mask(seq_segment, seq_keep, offset, block_rows)
            weights = jnp.exp(
                block_scores(block_queries, seq_keys, allowed)
                - seq_logsums[:, offset : offset + block_rows, None]
            )
            value_grad = value_grad + jnp.einsum(
                "hqk,qhd->khd",
                weights.astype(jnp.bfloat16),
                block_upstream,
                preferred_element_type=jnp.float32,
            )
            weight_grad = jnp.einsum(
                "qhd,khd->hqk", block_upstream, seq_values, preferred_element_type=jnp.float32
            )
            score_grad = (
                weights * (weight_grad - jnp.sum(weight_grad * weights, axis=-1, keepdims=True))
            ).astype(jnp.bfloat16)
            query_grads.append(
                jnp.einsum("hqk,khd->qhd", score_grad, seq_keys, preferred_element_type=jnp.float32)
                * score_scale
            )
            key_grad = (
                key_grad
                + jnp.einsum(
                    "hqk,qhd->khd", score_grad, block_queries, preferred_element_type=jnp.float32
                )
                * score_scale
            )
        return (state_carry, (jnp.concatenate(query_grads, axis=0), key_grad, value_grad))

    items = (
        queries.reshape(layout),
        key_rows.reshape(layout),
        value_rows.reshape(layout),
        segment_ids.reshape(sequences, LEN),
        keep_mask.reshape(sequences, LEN),
        logsums,
        upstream.reshape(layout),
    )
    unused, (query_back, key_back, value_back) = lax.scan(per_sequence, jnp.float32(0), items)
    return (
        query_back.reshape(row_count, channels),
        key_back.reshape(row_count, channels),
        value_back.reshape(row_count, channels),
    )


def spread(vector, row_devices):
    return jnp.broadcast_to(vector[:, None], (vector.shape[0], row_devices))


def local(
    inputs,
    segment_ids,
    keep_mask,
    query_weight,
    query_bias,
    key_weight,
    value_weight,
    value_bias,
    output_weight,
    output_bias,
    first_gain,
    first_shift,
    expand_weight,
    expand_bias,
    reduce_weight,
    reduce_bias,
    second_gain,
    second_shift,
    cotangent,
):
    inputs = as_rows(inputs)
    cotangent = as_rows(cotangent)
    query_full, key_full, value_full, output_full, expand_full, reduce_full = (
        lax.all_gather(query_weight, "row", axis=1, tiled=True),
        lax.all_gather(key_weight, "row", axis=1, tiled=True),
        lax.all_gather(value_weight, "row", axis=1, tiled=True),
        lax.all_gather(output_weight, "row", axis=1, tiled=True),
        lax.all_gather(expand_weight, "row", axis=1, tiled=True),
        lax.all_gather(reduce_weight, "row", axis=1, tiled=True),
    )
    queries = (forward_product(inputs, query_full) + query_bias).astype(jnp.bfloat16)
    key_rows = forward_product(inputs, key_full).astype(jnp.bfloat16)
    value_rows = (forward_product(inputs, value_full) + value_bias).astype(jnp.bfloat16)
    context, logsums = attention_forward(queries, key_rows, value_rows, segment_ids, keep_mask)
    context = context.astype(jnp.bfloat16)
    attended = lax.psum_scatter(
        forward_product(context, output_full).astype(jnp.bfloat16),
        "col",
        scatter_dimension=1,
        tiled=True,
    ).astype(jnp.float32)
    middle, first_normal, first_inverse = norm_forward(
        inputs.astype(jnp.float32) + attended + output_bias, first_gain, first_shift
    )
    middle_low = middle.astype(jnp.bfloat16)
    expanded = forward_product(middle_low, expand_full) + expand_bias
    activated = jax.nn.gelu(expanded, approximate=False).astype(jnp.bfloat16)
    reduced = forward_product(activated, reduce_full)
    result, second_normal, second_inverse = norm_forward(
        middle + reduced + reduce_bias, second_gain, second_shift
    )
    second_back, gain_second, shift_second = norm_backward(
        cotangent.astype(jnp.float32), second_normal, second_inverse, second_gain
    )
    bias_reduce = jnp.sum(second_back, axis=0)
    reduced_back = second_back.astype(jnp.bfloat16)
    activated_back = product_transposed(reduced_back, reduce_full)
    grad_reduce = product_over_rows(activated, reduced_back)
    gelu_slope = 0.5 * (1.0 + lax.erf(expanded * ROOT_HALF)) + expanded * DENSITY_SCALE * jnp.exp(
        -0.5 * expanded * expanded
    )
    expanded_back = (activated_back * gelu_slope).astype(jnp.bfloat16)
    bias_expand = jnp.sum(expanded_back.astype(jnp.float32), axis=0)
    grad_expand = product_over_rows(middle_low, expanded_back)
    middle_back = second_back + product_transposed(expanded_back, expand_full)
    first_back, gain_first, shift_first = norm_backward(
        middle_back, first_normal, first_inverse, first_gain
    )
    bias_output = jnp.sum(first_back, axis=0)
    attended_back = first_back.astype(jnp.bfloat16)
    upstream_whole = lax.all_gather(attended_back, "col", axis=1, tiled=True)
    context_grad = product_transposed(upstream_whole, output_full)
    grad_output = product_over_rows(context, upstream_whole)
    query_back, key_back, value_back = attention_backward(
        queries,
        key_rows,
        value_rows,
        segment_ids,
        keep_mask,
        logsums,
        context_grad.astype(jnp.bfloat16),
    )
    query_low = query_back.astype(jnp.bfloat16)
    key_low = key_back.astype(jnp.bfloat16)
    value_low = value_back.astype(jnp.bfloat16)
    bias_query = jnp.sum(query_low.astype(jnp.float32), axis=0)
    bias_value = jnp.sum(value_low.astype(jnp.float32), axis=0)
    grad_query = product_over_rows(inputs, query_low)
    grad_key = product_over_rows(inputs, key_low)
    grad_value = product_over_rows(inputs, value_low)
    input_grad = (
        first_back
        + product_transposed(query_low, query_full)
        + product_transposed(key_low, key_full)
        + product_transposed(value_low, value_full)
    )
    row_devices = lax.axis_size("row")
    scattered = (
        lax.psum_scatter(
            grad_query.astype(jnp.bfloat16), "row", scatter_dimension=1, tiled=True
        ).astype(jnp.float32),
        lax.psum_scatter(
            grad_key.astype(jnp.bfloat16), "row", scatter_dimension=1, tiled=True
        ).astype(jnp.float32),
        lax.psum_scatter(
            grad_value.astype(jnp.bfloat16), "row", scatter_dimension=1, tiled=True
        ).astype(jnp.float32),
        lax.psum_scatter(
            grad_output.astype(jnp.bfloat16), "row", scatter_dimension=1, tiled=True
        ).astype(jnp.float32),
        lax.psum_scatter(
            grad_expand.astype(jnp.bfloat16), "row", scatter_dimension=1, tiled=True
        ).astype(jnp.float32),
        lax.psum_scatter(
            grad_reduce.astype(jnp.bfloat16), "row", scatter_dimension=1, tiled=True
        ).astype(jnp.float32),
        lax.psum_scatter(
            spread(bias_query, row_devices).astype(jnp.bfloat16),
            "row",
            scatter_dimension=1,
            tiled=True,
        ).astype(jnp.float32),
        lax.psum_scatter(
            spread(bias_value, row_devices).astype(jnp.bfloat16),
            "row",
            scatter_dimension=1,
            tiled=True,
        ).astype(jnp.float32),
        lax.psum_scatter(
            spread(bias_output, row_devices).astype(jnp.bfloat16),
            "row",
            scatter_dimension=1,
            tiled=True,
        ).astype(jnp.float32),
        lax.psum_scatter(
            spread(gain_first, row_devices).astype(jnp.bfloat16),
            "row",
            scatter_dimension=1,
            tiled=True,
        ).astype(jnp.float32),
        lax.psum_scatter(
            spread(shift_first, row_devices).astype(jnp.bfloat16),
            "row",
            scatter_dimension=1,
            tiled=True,
        ).astype(jnp.float32),
        lax.psum_scatter(
            spread(bias_expand, row_devices).astype(jnp.bfloat16),
            "row",
            scatter_dimension=1,
            tiled=True,
        ).astype(jnp.float32),
        lax.psum_scatter(
            spread(bias_reduce, row_devices).astype(jnp.bfloat16),
            "row",
            scatter_dimension=1,
            tiled=True,
        ).astype(jnp.float32),
        lax.psum_scatter(
            spread(gain_second, row_devices).astype(jnp.bfloat16),
            "row",
            scatter_dimension=1,
            tiled=True,
        ).astype(jnp.float32),
        lax.psum_scatter(
            spread(shift_second, row_devices).astype(jnp.bfloat16),
            "row",
            scatter_dimension=1,
            tiled=True,
        ).astype(jnp.float32),
    )
    summed = (
        lax.psum(scattered[0].astype(jnp.bfloat16), "dp").astype(jnp.float32),
        lax.psum(scattered[1].astype(jnp.bfloat16), "dp").astype(jnp.float32),
        lax.psum(scattered[2].astype(jnp.bfloat16), "dp").astype(jnp.float32),
        lax.psum(scattered[3].astype(jnp.bfloat16), "dp").astype(jnp.float32),
        lax.psum(scattered[4].astype(jnp.bfloat16), "dp").astype(jnp.float32),
        lax.psum(scattered[5].astype(jnp.bfloat16), "dp").astype(jnp.float32),
        lax.psum(scattered[6][:, 0].astype(jnp.bfloat16), "dp").astype(jnp.float32),
        lax.psum(scattered[7][:, 0].astype(jnp.bfloat16), "dp").astype(jnp.float32),
        lax.psum(scattered[8][:, 0].astype(jnp.bfloat16), "dp").astype(jnp.float32),
        lax.psum(scattered[9][:, 0].astype(jnp.bfloat16), "dp").astype(jnp.float32),
        lax.psum(scattered[10][:, 0].astype(jnp.bfloat16), "dp").astype(jnp.float32),
        lax.psum(scattered[11][:, 0].astype(jnp.bfloat16), "dp").astype(jnp.float32),
        lax.psum(scattered[12][:, 0].astype(jnp.bfloat16), "dp").astype(jnp.float32),
        lax.psum(scattered[13][:, 0].astype(jnp.bfloat16), "dp").astype(jnp.float32),
        lax.psum(scattered[14][:, 0].astype(jnp.bfloat16), "dp").astype(jnp.float32),
    )
    return (
        as_pairs(result.astype(jnp.bfloat16)),
        as_pairs(input_grad),
        summed[0],
        summed[6],
        summed[1],
        summed[2],
        summed[7],
        summed[3],
        summed[8],
        summed[9],
        summed[10],
        summed[4],
        summed[11],
        summed[5],
        summed[12],
        summed[13],
        summed[14],
    )


def solution(mesh):
    placed = (
        P(("dp", "row"), "col", None),
        P(("dp", "row")),
        P(("dp", "row")),
        P("col", "row"),
        P("col"),
        P("col", "row"),
        P("col", "row"),
        P("col"),
        P("col", "row"),
        P("col"),
        P("col"),
        P("col"),
        P("col", "row"),
        P("col"),
        P("col", "row"),
        P("col"),
        P("col"),
        P("col"),
        P(("dp", "row"), "col", None),
    )
    return jax.shard_map(
        local,
        mesh=mesh,
        in_specs=placed,
        out_specs=(
            P(("dp", "row"), "col", None),
            P(("dp", "row"), "col", None),
            P("col", "row"),
            P("col"),
            P("col", "row"),
            P("col", "row"),
            P("col"),
            P("col", "row"),
            P("col"),
            P("col"),
            P("col"),
            P("col", "row"),
            P("col"),
            P("col", "row"),
            P("col"),
            P("col"),
            P("col"),
        ),
        check_vma=False,
    )
```

profile of v0, /device:TPU:0, one launch (start us, length us, event | category | flops | bytes accessed | tf_op | source)
XLA Modules:
  0.0 665.8 jit_solution(17012676582966933652)
XLA Ops:
  8.7 6.6 all_gather.22
  15.2 5.8 all_gather.23
  21.0 5.5 all_gather.21
  27.6 6.7 %all_gather.24 = bf16[192,768]{0,1:T(8,128)(2,1)S(1)} all-gather(bf16[192,192]{0,1:T(8,128)(2,1)S(1)} %copy.64), channel_id=1, replica_groups=mesh['dp'=2,'row'=4,'col'=4] {'row'}, dimensions={1}, use_global_device_ids=true | all-gather | bytes 368640 | tf_op jit(solution)/shard_map/all_gather | solution.py:206
  58.3 39.8 %while.26 = (s32[]{:T(128)}, bf16[3,1024,3,64]{1,3,2,0:T(8,128)(2,1)}, f32[3,3,1024]{2,1,0:T(4,128)S(1)}, bf16[3,1024,3,64]{1,3,2,0:T(8,128)(2,1)}, s32[3,1024]{...) while((s32[]{:T(128)}, ...), condition=%wide.region_5.6_spmd, body=%wide.region_0.5_spmd.sunk | while | flops 848037376 | bytes 49984188 | solution.py:105
  114.8 7.0 %all_gather.25 = bf16[192,768]{0,1:T(8,128)(2,1)} all-gather(bf16[192,192]{0,1:T(8,128)(2,1)S(1)} %copy.65), channel_id=1, replica_groups=mesh['dp'=2,'row'=4,'col'=4] {'row'}, dimensions={1}, use_global_device_ids=true | all-gather | bytes 368640 | tf_op jit(solution)/shard_map/all_gather | solution.py:207
  121.8 6.0 all_gather.26
  127.8 64.6 %reduce-scatter.12.cloned.1.call-done = bf16[3072,192]{0,1:T(8,128)(2,1)} async-done(((bf16[3072,768]{0,1:T(8,128)(2,1)}), bf16[3072,192]{0,1:T(8,128)(2,1)}) %reduce-scatter.12.cloned.1.call-update) | async-done | bytes 1179664 | tf_op jit(solution)/shard_map/reduce_scatter | solution.py:215
  194.6 18.2 %all-reduce.12 = (f32[3072]{0:T(1024)S(1)}, f32[3072]{0:T(1024)S(1)}) all-reduce(f32[3072]{0:T(1024)S(1)} %get-tuple-element.221, f32[3072]{0:T(1024)S(1)} %get-tuple-element.220), channel_id=1, replica_groups=mesh['dp'=2,'row'=4,'col'=4] {'col'}, use_global_device_ids=true, to_apply=%region_10.11 | all-reduce | flops 6144 | bytes 49152 | tf_op jit(solution)/shard_map/psum | solution.py:42
  212.9 24.4 %fusion.92 = (bf16[3072,768]{1,0:T(8,128)(2,1)S(1)}, f32[3072,768]{1,0:T(8,128)}) fusion(f32[768]{0:T(1024)S(1)} %copy-done.49, bf16[192,768]{0,1:T(8,128)(2,1)} %all_gather.25, f32[192]{0:T(256)S(1)} %copy-done.51, f32[192]{0:T(256)S(1)} %copy-done.45, f32[3072]{0:T(1024)S(1)} %get-tuple-element.325, f32[3072]{0:T(1024)S(1)} %get-tuple-element.324, ...), kind=kOutput, calls=%fused_computation.125 | convolution fusion | flops 1066991616 | bytes 16839936 | tf_op jit(solution)/shard_map/dot_general | solution.py:26
  240.6 15.8 %all-reduce.11 = (f32[3072]{0:T(1024)S(1)}, f32[3072]{0:T(1024)S(1)}) all-reduce(f32[3072]{0:T(1024)S(1)} %get-tuple-element.224, f32[3072]{0:T(1024)S(1)} %get-tuple-element.223), channel_id=1, replica_groups=mesh['dp'=2,'row'=4,'col'=4] {'col'}, use_global_device_ids=true, to_apply=%region_14.15 | all-reduce | flops 6144 | bytes 49152 | tf_op jit(solution)/shard_map/psum | solution.py:42
  259.0 28.1 %all-reduce.10 = (f32[3072]{0:T(1024)S(1)}, f32[3072]{0:T(1024)S(1)}) all-reduce(f32[3072]{0:T(1024)S(1)} %get-tuple-element.226, f32[3072]{0:T(1024)S(1)} %get-tuple-element.225), channel_id=1, replica_groups=mesh['dp'=2,'row'=4,'col'=4] {'col'}, use_global_device_ids=true, to_apply=%region_18.19 | all-reduce | flops 6144 | bytes 49152 | tf_op jit(solution)/shard_map/psum | solution.py:51
  287.1 9.1 %fusion.139 = (bf16[768]{0:T(1024)(128)(2,1)}, bf16[3072,768]{1,0:T(8,128)(2,1)S(1)}) fusion(f32[3072,768]{1,0:T(8,128)} %get-tuple-element.327, f32[768]{0:T(1024)S(1)} %copy-done.49, bf16[768,192]{0,1:T(8,128)(2,1)S(1)} %all_gather.26, f32[3072]{0:T(1024)S(1)} %get-tuple-element.267, f32[3072,192]{0,1:T(8,128)} %get-tuple-element.328, ...), kind=kOutput, calls=%fused_computation.220 | convolution fusion | flops 940178688 | bytes 18044160 | tf_op jit(solution)/shard_map/dot_general | solution.py:30
  296.3 5.0 multiply_reduce_fusion.2
  301.3 15.8 %all-reduce.9 = (f32[3072]{0:T(1024)S(1)}, f32[3072]{0:T(1024)S(1)}) all-reduce(f32[3072]{0:T(1024)S(1)} %get-tuple-element.216, f32[3072]{0:T(1024)S(1)} %get-tuple-element.219), channel_id=1, replica_groups=mesh['dp'=2,'row'=4,'col'=4] {'col'}, use_global_device_ids=true, to_apply=%region_22.23 | all-reduce | flops 6144 | bytes 49152 | tf_op jit(solution)/shard_map/psum | solution.py:51
  326.9 4.5 convolution_convert_fusion.4
  332.4 5.5 fusion.114
  344.1 68.9 %all-gather.2.cloned.1.call-done = bf16[3072,768]{0,1:T(8,128)(2,1)} async-done(((bf16[3072,192]{0,1:T(8,128)(2,1)}), bf16[3072,768]{0,1:T(8,128)(2,1)}) %all-gather.2.cloned.1.call-update) | async-done | bytes 4718608 | tf_op jit(solution)/shard_map/all_gather | solution.py:250
  413.0 4.4 convolution_convert_fusion.5
  418.4 5.8 convolution_convert_fusion.3
  424.3 10.4 %reduce-scatter.24.cloned.1.call-done = bf16[192,192]{1,0:T(8,128)(2,1)} async-done(((bf16[768,192]{1,0:T(8,128)(2,1)}), bf16[192,192]{1,0:T(8,128)(2,1)}) %reduce-scatter.24.cloned.1.call-update) | async-done | bytes 73744
  436.4 4.5 convolution_convert_fusion.1
  451.7 100.7 %while.27 = (s32[]{:T(128)}, bf16[3,1024,3,64]{1,3,2,0:T(8,128)(2,1)}, bf16[3,1024,3,64]{1,3,2,0:T(8,128)(2,1)}, bf16[3,1024,3,64]{1,3,2,0:T(8,128)(2,1)}, bf16[...) while((s32[]{:T(128)}, ...), condition=%wide.region_26.27_spmd, body=%wide.region_23.26_spmd.sunk | while | flops 2066414080 | bytes 160987104 | solution.py:167
  459.8 4.3 multiply_reduce_fusion.9
  468.4 7.8 %multiply_convert_fusion.3 = (bf16[3,512,1024]{2,1,0:T(8,128)(2,1)}, bf16[3,512,1024]{2,1,0:T(8,128)(2,1)S(1)}) fusion(f32[3,512,1024]{2,1,0:T(8,128)} %get-tuple-element.492, f32[3,512,1024]{2,1,0:T(8,128)S(1)} %fusion.227, f32[3,512]{1,0:T(4,128)S(1)} %get-tuple-element.493, f32[3,512]{1,0:T(4,128)S(1)} %get-tuple-element.488, ...), kind=kLoop, calls=%fused_computation.50.clone.1 | loop fusion | flops 18874368 | bytes 32530432 | tf_op jit(solution)/shard_map/while/body/eval_jaxpr/convert_element_type | solution.py:144
  501.8 7.8 %multiply_convert_fusion.3 = (bf16[3,512,1024]{2,1,0:T(8,128)(2,1)}, bf16[3,512,1024]{2,1,0:T(8,128)(2,1)S(1)}) fusion(f32[3,512,1024]{2,1,0:T(8,128)} %get-tuple-element.492, f32[3,512,1024]{2,1,0:T(8,128)S(1)} %fusion.227, f32[3,512]{1,0:T(4,128)S(1)} %get-tuple-element.493, f32[3,512]{1,0:T(4,128)S(1)} %get-tuple-element.488, ...), kind=kLoop, calls=%fused_computation.50.clone.1 | loop fusion | flops 18874368 | bytes 32530432 | tf_op jit(solution)/shard_map/while/body/eval_jaxpr/convert_element_type | solution.py:144
  526.6 4.3 multiply_reduce_fusion.9
  535.2 7.8 %multiply_convert_fusion.3 = (bf16[3,512,1024]{2,1,0:T(8,128)(2,1)}, bf16[3,512,1024]{2,1,0:T(8,128)(2,1)S(1)}) fusion(f32[3,512,1024]{2,1,0:T(8,128)} %get-tuple-element.492, f32[3,512,1024]{2,1,0:T(8,128)S(1)} %fusion.227, f32[3,512]{1,0:T(4,128)S(1)} %get-tuple-element.493, f32[3,512]{1,0:T(4,128)S(1)} %get-tuple-element.488, ...), kind=kLoop, calls=%fused_computation.50.clone.1 | loop fusion | flops 18874368 | bytes 32530432 | tf_op jit(solution)/shard_map/while/body/eval_jaxpr/convert_element_type | solution.py:144
  588.6 10.3 %all-reduce.13 = (bf16[192,4]{0,1:T(4,128)(2,1)S(1)}, bf16[192,4]{0,1:T(4,128)(2,1)S(1)}, bf16[192,4]{0,1:T(4,128)(2,1)S(1)}, bf16[192,4]{0,1:T(4,128)(2,1)S(1)}...) all-reduce(bf16[192,4]{0,1:T(4,128)(2,1)S(1)} %broadcast_in_dim.102, ...), channel_id=4, replica_groups=mesh['dp'=2,'row'=4,'col'=4] {'row'}, use_global_device_ids=true, to_apply=%region_30.31.clone | all-reduce | flops 9216 | bytes 36864
  605.1 22.6 %reduce-scatter.16.cloned.1.call-done = bf16[192,48]{0,1:T(8,128)(2,1)} async-done(((bf16[192,192]{0,1:T(8,128)(2,1)}), bf16[192,48]{0,1:T(8,128)(2,1)}) %reduce-scatter.16.cloned.1.call-update) | async-done | bytes 18448 | tf_op jit(solution)/shard_map/reduce_scatter | solution.py:281
  627.8 10.1 %all-reduce.14 = (bf16[192,48]{0,1:T(8,128)(2,1)S(1)}, bf16[192]{0:T(256)(128)(2,1)S(1)}, bf16[192,48]{0,1:T(8,128)(2,1)S(1)}, bf16[192,48]{0,1:T(8,128)(2,1)S(1...) all-reduce(bf16[192,48]{0,1:T(8,128)(2,1)} %reduce-scatter.14.clone, ...), channel_id=1, replica_groups=mesh['dp'=2,'row'=4,'col'=4] {'dp'}, use_global_device_ids=true, to_apply=%region_28.29 | all-reduce | flops 29952 | bytes 119808 | tf_op jit(solution)/shard_map/psum | solution.py:352
  644.8 9.5 %all-reduce.18.cloned.1.call-done = (bf16[192,192]{1,0:T(8,128)(2,1)}, bf16[192,192]{1,0:T(8,128)(2,1)}, bf16[768,48]{0,1:T(8,128)(2,1)}) async-done(((bf16[192,192]{1,0:T(8,128)(2,1)}, bf16[192,192]{1,0:T(8,128)(2,1)}, bf16[768,48]{0,1:T(8,128)(2,1)}), (bf16[192,192]{1,0:T(8,128)(2,1)}, bf16[192,192]{1,0:T(8,128)(2,1)}, bf16[768,48]{0,1:T(8,128)(2,1)})) %all-reduce.18.cloned.1.call-update) | async-done | bytes 221200 | tf_op jit(solution)/shard_map/psum | solution.py:355
  (361 shorter events, 242.5 us)
Async XLA Ops:
  7.2 185.2 %reduce-scatter.12.cloned.1.call-start = ((), (), s32[]{:S(2)}) async-start(), calls=%async_computation.7 | async-start | bytes 5898240 | tf_op jit(solution)/shard_map/reduce_scatter | solution.py:215
  15.2 27.6 %copy-start.31 = (bf16[192,192]{0,1:T(8,128)(2,1)}, bf16[192,192]{0,1:T(8,128)(2,1)S(1)}, u32[]{:S(2)}) copy-start(bf16[192,192]{0,1:T(8,128)(2,1)S(1)} %all_gather.22) | copy-start | bytes 221188
  21.0 16.6 %copy-start.27 = (bf16[192,192]{0,1:T(8,128)(2,1)}, bf16[192,192]{0,1:T(8,128)(2,1)S(1)}, u32[]{:S(2)}) copy-start(bf16[192,192]{0,1:T(8,128)(2,1)S(1)} %all_gather.23) | copy-start | bytes 221188
  26.5 21.8 %copy-start.29 = (bf16[192,192]{0,1:T(8,128)(2,1)}, bf16[192,192]{0,1:T(8,128)(2,1)S(1)}, u32[]{:S(2)}) copy-start(bf16[192,192]{0,1:T(8,128)(2,1)S(1)} %all_gather.21) | copy-start | bytes 221188
  43.5 4.8 copy-start.44
  105.6 307.4 %all-gather.2.cloned.1.call-start = ((), (), s32[]{:S(2)}) async-start(), calls=%async_computation.8 | async-start | bytes 5898240 | tf_op jit(solution)/shard_map/all_gather | solution.py:250
  108.3 13.5 %copy-start.35 = (bf16[768,48]{0,1:T(8,128)(2,1)S(1)}, bf16[768,48]{0,1:T(8,128)(2,1)}, u32[]{:S(2)}) copy-start(bf16[768,48]{0,1:T(8,128)(2,1)} %param.37) | copy-start | bytes 221188
  111.9 80.5 %copy-start.36 = (f32[192]{0:T(256)S(1)}, f32[192]{0:T(256)}, u32[]{:S(2)}) copy-start(f32[192]{0:T(256)} %param.32) | copy-start | bytes 2308
  111.9 100.9 %copy-start.45 = (f32[192]{0:T(256)S(1)}, f32[192]{0:T(256)}, u32[]{:S(2)}) copy-start(f32[192]{0:T(256)} %param.33) | copy-start | bytes 2308
  111.9 100.9 %copy-start.49 = (f32[768]{0:T(1024)S(1)}, f32[768]{0:T(1024)}, u32[]{:S(2)}) copy-start(f32[768]{0:T(1024)} %param.36) | copy-start | bytes 9220
  111.9 100.9 %copy-start.51 = (f32[192]{0:T(256)S(1)}, f32[192]{0:T(256)}, u32[]{:S(2)}) copy-start(f32[192]{0:T(256)} %param.34) | copy-start | bytes 2308
  212.8 24.5 %copy-start.15 = (bf16[3072,192]{0,1:T(8,128)(2,1)S(1)}, bf16[3072,192]{0,1:T(8,128)(2,1)}, u32[]{:S(2)}) copy-start(bf16[3072,192]{0,1:T(8,128)(2,1)} %copy.59) | copy-start | bytes 3538948
  212.8 24.5 %copy-start.22 = (bf16[3072,192]{0,1:T(8,128)(2,1)S(1)}, bf16[3072,192]{0,1:T(8,128)(2,1)}, u32[]{:S(2)}) copy-start(bf16[3072,192]{0,1:T(8,128)(2,1)} %reduce-scatter.12.cloned.1.call-done) | copy-start | bytes 3538948
  212.8 24.5 %copy-start.50 = (f32[192]{0:T(256)S(1)}, f32[192]{0:T(256)}, u32[]{:S(2)}) copy-start(f32[192]{0:T(256)} %param.38) | copy-start | bytes 2308
  237.3 19.1 %copy-start.37 = (f32[192]{0:T(256)S(1)}, f32[192]{0:T(256)}, u32[]{:S(2)}) copy-start(f32[192]{0:T(256)} %param.39) | copy-start | bytes 2308
  287.1 9.1 %copy-start.16 = (bf16[3072,192]{0,1:T(8,128)(2,1)S(1)}, bf16[3072,192]{0,1:T(8,128)(2,1)}, u32[]{:S(2)}) copy-start(bf16[3072,192]{0,1:T(8,128)(2,1)} %copy.59) | copy-start | bytes 3538948
  287.1 9.1 %copy-start.17 = (bf16[3072,192]{0,1:T(8,128)(2,1)S(1)}, bf16[3072,192]{0,1:T(8,128)(2,1)}, u32[]{:S(2)}) copy-start(bf16[3072,192]{0,1:T(8,128)(2,1)} %copy.67) | copy-start | bytes 3538948
  287.1 9.1 %copy-start.20 = (f32[3072,192]{0,1:T(8,128)S(1)}, f32[3072,192]{0,1:T(8,128)}, u32[]{:S(2)}) copy-start(f32[3072,192]{0,1:T(8,128)} %get-tuple-element.328) | copy-start | bytes 7077892
  287.1 9.1 %copy-start.23 = (bf16[3072,192]{0,1:T(8,128)(2,1)S(1)}, bf16[3072,192]{0,1:T(8,128)(2,1)}, u32[]{:S(2)}) copy-start(bf16[3072,192]{0,1:T(8,128)(2,1)} %reduce-scatter.12.cloned.1.call-done) | copy-start | bytes 3538948
  287.1 9.1 %copy-start.33 = (bf16[192,768]{0,1:T(8,128)(2,1)S(1)}, bf16[192,768]{0,1:T(8,128)(2,1)}, u32[]{:S(2)}) copy-start(bf16[192,768]{0,1:T(8,128)(2,1)} %all_gather.25) | copy-start | bytes 884740
  296.2 5.1 copy-start.54
  323.9 110.9 %reduce-scatter.24.cloned.1.call-start = ((), (), s32[]{:S(2)}) async-start(), calls=%async_computation.14 | async-start | bytes 491520
  326.9 5.6 copy-start.46
  332.4 244.5 %reduce-scatter.22.cloned.1.call-start = ((), (), s32[]{:S(2)}) async-start(), calls=%async_computation.13 | async-start | bytes 491520
  418.4 160.1 %reduce-scatter.20.cloned.1.call-start = ((), (), s32[]{:S(2)}) async-start(), calls=%async_computation.12 | async-start | bytes 368640 | tf_op jit(solution)/shard_map/reduce_scatter | solution.py:293
  424.3 178.0 %reduce-scatter.14.cloned.1.call-start = ((), (), s32[]{:S(2)}) async-start(), calls=%async_computation.9 | async-start | bytes 122880 | tf_op jit(solution)/shard_map/reduce_scatter | solution.py:278
  453.7 6.1 copy-start.1
  487.1 6.1 copy-start.1
  520.5 6.1 copy-start.1
  563.2 41.9 %reduce-scatter.18.cloned.1.call-start = ((), (), s32[]{:S(2)}) async-start(), calls=%async_computation.11 | async-start | bytes 122880 | tf_op jit(solution)/shard_map/reduce_scatter | solution.py:284
  569.6 58.2 %reduce-scatter.16.cloned.1.call-start = ((), (), s32[]{:S(2)}) async-start(), calls=%async_computation.10 | async-start | bytes 122880 | tf_op jit(solution)/shard_map/reduce_scatter | solution.py:281
  572.1 82.3 %all-reduce.18.cloned.1.call-start = ((), (), s32[]{:S(2)}) async-start(), calls=%async_computation.15 | async-start | bytes 540672 | tf_op jit(solution)/shard_map/psum | solution.py:355
  (54 other events, 146.5 us)
Sparse Core Ops, SparseCore 0:
  105.7 86.6 reduce-scatter.11
  324.0 88.9 all-gather.1
  415.5 19.2 reduce-scatter.23
  437.1 20.8 reduce-scatter.21
  460.3 20.2 reduce-scatter.19
  563.3 19.6 reduce-scatter.13
  585.5 19.6 reduce-scatter.17
  608.1 19.5 reduce-scatter.15
  630.8 23.5 all-reduce.17
where the time goes:
time: 677 us; the launch traced here: 666 us
  waiting for transfers between devices  179 us (26%)
  matrix products  173 us (26%)
  blocking collectives  136 us (20%)
  local copies, waits for them, and re-layouts  83.8 us (12%)
  other arithmetic  77.8 us (11%)
  between operations  14.7 us (2%)
    all_gather x1, waiting for transfers between devices, local(): upstream_whole = lax.all_gather(attended_back, 'col', axis=1, tiled=True)  68.9 us
    reduce_scatter x1, waiting for transfers between devices, local(): lax.psum_scatter(forward_product(context, output_full).astype(jnp.bfloat1...  64.6 us
    psum x2, blocking collectives, norm_backward(): lax.psum((jnp.sum(scaled, axis=1), jnp.sum(scaled * normal, axis=1)), 'col')  43.8 us
    dot_general x6, matrix products, forward_product(): return jnp.dot(left, right, preferred_element_type=jnp.float32)  34.3 us
    psum x2, blocking collectives, norm_forward(): lax.psum((jnp.sum(summed, axis=1), jnp.sum(summed * summed, axis=1)), 'col')  33.9 us
    dot_general x6, matrix products, product_transposed(): lax.dot_general(left, right, (((1,), (1,)), ((), ())), preferred_element_...  30.2 us
    dot_general x6, matrix products, per_sequence(): jnp.einsum('qhd,khd->hqk', block_upstream, seq_values, preferred_element_...  25.7 us
    convert_element_type x3, other arithmetic, per_sequence(): score_grad = (weights * (weight_grad - jnp.sum(weight_grad * weights, axi...  23.4 us
  transfers between devices with their start and end apart: 9, of which 6 were waited for; matrix products, arithmetic and copies ran while one was open for 30% of the time, Pallas kernels for 0%

commit v1 on v0

--- a/solution.py
+++ b/solution.py
@@ -1,17 +1,332 @@
+import functools
+
 import jax
 import jax.numpy as jnp
 from jax import lax
+from jax.experimental import pallas as pl
+from jax.experimental.pallas import tpu as pltpu
 from jax.sharding import PartitionSpec as P
+
+MESH = pl.DeviceIdType.MESH
+BF16 = jnp.bfloat16
+F32 = jnp.float32
 
 D = 768
 HEAD_DIM = 64
 LEN = 1024
-
-
+BLOCK = 256
+PAIRS = BLOCK // 2
 EPSILON = 1e-05
 NEGATIVE = -1e30
 ROOT_HALF = 0.7071067811865476
 DENSITY_SCALE = 0.3989422804014327
+VMEM_BYTES = 62 * 1024 * 1024
+
+
+def dot(left, right):
+    return jnp.dot(left, right, preferred_element_type=F32)
+
+
+def dot_nt(left, right):
+    return lax.dot_general(left, right, (((1,), (1,)), ((), ())), preferred_element_type=F32)
+
+
+def columns_of(pairs):
+    width = pairs.shape[1] // 2
+    turned = pairs.T
+    return jnp.concatenate([turned[:width], turned[width:]], axis=1)
+
+
+def pairs_of(columns):
+    half = columns.shape[1] // 2
+    return jnp.concatenate([columns[:, :half], columns[:, half:]], axis=0).T
+
+
+def vmem_spec():
+    return pl.BlockSpec(memory_space=pltpu.VMEM)
+
+
+def key_range(segment_ref, keep_ref, base, query_block, blocks):
+    first = segment_ref[base + query_block * BLOCK]
+    last = segment_ref[base + query_block * BLOCK + BLOCK - 1]
+    low = jnp.int32(0)
+    high = jnp.int32(-1)
+    real = jnp.int32(-1)
+    for block in range(blocks):
+        low += (segment_ref[base + block * BLOCK + BLOCK - 1] < first).astype(jnp.int32)
+        high += (segment_ref[base + block * BLOCK] <= last).astype(jnp.int32)
+        real += (keep_ref[base + block * BLOCK] == 1).astype(jnp.int32)
+    return low, jnp.minimum(high, jnp.maximum(real, query_block))
+
+
+def block_bias(key_codes, codes_ref, query_block, key_block):
+    keys = key_codes[pl.ds(pl.multiple_of(key_block * BLOCK, BLOCK), BLOCK), :]
+    keys = jnp.concatenate([keys, keys], axis=1)
+    queries = codes_ref[query_block, 0:1, :]
+    place = lax.broadcasted_iota(jnp.int32, (BLOCK, BLOCK), 0) - lax.broadcasted_iota(
+        jnp.int32, (BLOCK, BLOCK), 1
+    )
+    same = place == (query_block - key_block) * BLOCK
+    return jnp.where((keys == queries) | same, 0.0, NEGATIVE)
+
+
+def spread_key_codes(codes_ref, key_codes, blocks):
+    for block in range(blocks):
+        column = codes_ref[block].T[:, 1:2]
+        key_codes[pl.ds(block * BLOCK, BLOCK), :] = jnp.broadcast_to(column, (BLOCK, 128))
+
+
+def forward_kernel(
+    segment_ref, keep_ref, inputs_ref, weight_ref, vectors_ref, codes_ref,
+    turned_ref, joined_ref, context_ref, logsum_ref,
+    key_codes, key_rows, value_rows, scaled, scores, totals, vector_columns,
+):
+    blocks = LEN // BLOCK
+    base = pl.program_id(0) * LEN
+    width = inputs_ref.shape[1] // 2
+    heads = width // HEAD_DIM
+    vector_columns[...] = vectors_ref[...].T
+    spread_key_codes(codes_ref, key_codes, blocks)
+    for block in range(blocks):
+        turned = columns_of(inputs_ref[block * PAIRS : (block + 1) * PAIRS, :])
+        turned_ref[block] = turned
+        query = (dot(weight_ref[0], turned) + vector_columns[:, 0:1]).astype(BF16)
+        key = dot(weight_ref[1], turned).astype(BF16)
+        value = (dot(weight_ref[2], turned) + vector_columns[:, 1:2]).astype(BF16)
+        joined_ref[block, 0] = query
+        joined_ref[block, 1] = key
+        joined_ref[block, 2] = value
+        scaled[block] = query * jnp.array(HEAD_DIM ** (-0.5), BF16)
+        for head in range(heads):
+            rows = slice(head * HEAD_DIM, (head + 1) * HEAD_DIM)
+            key_rows[head, block] = key[rows].T
+            value_rows[head, block, :HEAD_DIM] = value[rows]
+            value_rows[head, block, HEAD_DIM:] = jnp.ones((16, BLOCK), BF16)
+
+    def query_step(query_block, carry):
+        low, high = key_range(segment_ref, keep_ref, base, query_block, blocks)
+
+        def score_step(key_block, highest):
+            bias = block_bias(key_codes, codes_ref, query_block, key_block)
+            fresh = []
+            for head in range(heads):
+                rows = slice(head * HEAD_DIM, (head + 1) * HEAD_DIM)
+                score = dot(key_rows[head, key_block], scaled[query_block, rows, :]) + bias
+                scores[head, key_block] = score
+                fresh.append(
+                    jnp.maximum(
+                        highest[head], jnp.max(score.reshape(BLOCK // 8, 8, BLOCK), axis=0)
+                    )
+                )
+            return tuple(fresh)
+
+        start = jnp.full((8, BLOCK), 2 * NEGATIVE, F32)
+        highest = lax.fori_loop(low, high + 1, score_step, (start,) * heads)
+        highest = [jnp.max(part, axis=0, keepdims=True) for part in highest]
+        totals[...] = jnp.zeros_like(totals)
+
+        def value_step(key_block, carry):
+            for head in range(heads):
+                weights = jnp.exp(scores[head, key_block] - highest[head]).astype(BF16)
+                totals[head] += dot(value_rows[head, key_block], weights)
+            return carry
+
+        lax.fori_loop(low, high + 1, value_step, 0)
+        for head in range(heads):
+            rows = slice(head * HEAD_DIM, (head + 1) * HEAD_DIM)
+            total = totals[head, HEAD_DIM : HEAD_DIM + 1, :]
+            context_ref[query_block, rows, :] = (totals[head, :HEAD_DIM, :] / total).astype(BF16)
+            logsum_ref[query_block, head : head + 1, :] = highest[head] + jnp.log(total)
+        return carry
+
+    lax.fori_loop(0, blocks, query_step, 0)
+
+
+def attention_forward(pairs, segment_ids, keep_mask, weight, vectors, codes):
+    pair_count, doubled = pairs.shape
+    width = doubled // 2
+    heads = width // HEAD_DIM
+    sequences = pair_count * 2 // LEN
+    blocks = LEN // BLOCK
+    every = sequences * blocks
+
+    def whole(*shape):
+        return pl.BlockSpec(shape, lambda i, *refs: (0,) * len(shape))
+
+    def part(*shape):
+        return pl.BlockSpec(shape, lambda i, *refs: (i,) + (0,) * (len(shape) - 1))
+
+    return pl.pallas_call(
+        forward_kernel,
+        out_shape=(
+            jax.ShapeDtypeStruct((every, width, BLOCK), BF16),
+            jax.ShapeDtypeStruct((every, 3, width, BLOCK), BF16),
+            jax.ShapeDtypeStruct((every, width, BLOCK), BF16),
+            jax.ShapeDtypeStruct((every, 8, BLOCK), F32),
+        ),
+        grid_spec=pltpu.PrefetchScalarGridSpec(
+            num_scalar_prefetch=2,
+            grid=(sequences,),
+            in_specs=[
+                part(LEN // 2, doubled),
+                whole(3, width, width),
+                whole(*vectors.shape),
+                part(blocks, 8, BLOCK),
+            ],
+            out_specs=(
+                part(blocks, width, BLOCK),
+                part(blocks, 3, width, BLOCK),
+                part(blocks, width, BLOCK),
+                part(blocks, 8, BLOCK),
+            ),
+            scratch_shapes=[
+                pltpu.VMEM((LEN, 128), F32),
+                pltpu.VMEM((heads, blocks, BLOCK, HEAD_DIM), BF16),
+                pltpu.VMEM((heads, blocks, HEAD_DIM + 16, BLOCK), BF16),
+                pltpu.VMEM((blocks, width, BLOCK), BF16),
+                pltpu.VMEM((heads, blocks, BLOCK, BLOCK), F32),
+                pltpu.VMEM((heads, HEAD_DIM + 16, BLOCK), F32),
+                pltpu.VMEM((width, vectors.shape[0]), F32),
+            ],
+        ),
+        compiler_params=pltpu.CompilerParams(vmem_limit_bytes=VMEM_BYTES),
+        name="attention_forward",
+    )(segment_ids, keep_mask, pairs, weight, vectors, codes)
+
+
+def backward_kernel(
+    segment_ref, keep_ref, turned_ref, joined_ref, context_ref, logsum_ref, upstream_ref,
+    first_back_ref, weight_ref, codes_ref,
+    input_grad_ref, weight_grad_ref, bias_grad_ref,
+    key_codes, key_rows, value_rows, scaled, deltas, query_sum, key_sum, value_sum, weight_in,
+):
+    blocks = LEN // BLOCK
+    step = pl.program_id(0)
+    base = step * LEN
+    width = turned_ref.shape[1]
+    heads = width // HEAD_DIM
+    scale = HEAD_DIM ** (-0.5)
+
+    @pl.when(step == 0)
+    def start():
+        weight_grad_ref[...] = jnp.zeros_like(weight_grad_ref)
+        bias_grad_ref[...] = jnp.zeros_like(bias_grad_ref)
+        for kind in range(3):
+            weight_in[kind] = weight_ref[kind].T
+
+    spread_key_codes(codes_ref, key_codes, blocks)
+    query_sum[...] = jnp.zeros_like(query_sum)
+    key_sum[...] = jnp.zeros_like(key_sum)
+    value_sum[...] = jnp.zeros_like(value_sum)
+    for block in range(blocks):
+        query = joined_ref[block, 0]
+        scaled[block] = query * jnp.array(scale, BF16)
+        product = upstream_ref[block].astype(F32) * context_ref[block].astype(F32)
+        for head in range(heads):
+            rows = slice(head * HEAD_DIM, (head + 1) * HEAD_DIM)
+            key_rows[head, block] = joined_ref[block, 1, rows, :].T
+            value_rows[head, block] = joined_ref[block, 2, rows, :].T
+            deltas[block, head : head + 1, :] = jnp.sum(product[rows], axis=0, keepdims=True)
+
+    def query_step(query_block, carry):
+        low, high = key_range(segment_ref, keep_ref, base, query_block, blocks)
+
+        def key_step(key_block, carry):
+            bias = block_bias(key_codes, codes_ref, query_block, key_block)
+            for head in range(heads):
+                rows = slice(head * HEAD_DIM, (head + 1) * HEAD_DIM)
+                query = scaled[query_block, rows, :]
+                upstream = upstream_ref[query_block, rows, :]
+                logsum = logsum_ref[query_block, head : head + 1, :]
+                delta = deltas[query_block, head : head + 1, :]
+                weights = jnp.exp(dot(key_rows[head, key_block], query) + bias - logsum)
+                weight_back = dot(value_rows[head, key_block], upstream)
+                score_back = (weights * (weight_back - delta)).astype(BF16)
+                value_sum[key_block, rows, :] += dot_nt(upstream, weights.astype(BF16))
+                key_sum[key_block, rows, :] += dot_nt(query, score_back)
+                query_sum[query_block, rows, :] += dot(
+                    joined_ref[key_block, 1, rows, :], score_back
+                )
+            return carry
+
+        return lax.fori_loop(low, high + 1, key_step, carry)
+
+    lax.fori_loop(0, blocks, query_step, 0)
+    for block in range(blocks):
+        query_low = (query_sum[block] * scale).astype(BF16)
+        key_low = key_sum[block].astype(BF16)
+        value_low = value_sum[block].astype(BF16)
+        turned = turned_ref[block]
+        weight_grad_ref[0] += dot_nt(query_low, turned)
+        weight_grad_ref[1] += dot_nt(key_low, turned)
+        weight_grad_ref[2] += dot_nt(value_low, turned)
+        query_wide = query_low.astype(F32)
+        value_wide = value_low.astype(F32)
+        bias_grad_ref[0] += query_wide[:, :128] + query_wide[:, 128:]
+        bias_grad_ref[1] += value_wide[:, :128] + value_wide[:, 128:]
+        input_grad = (
+            first_back_ref[block]
+            + dot(weight_in[0], query_low)
+            + dot(weight_in[1], key_low)
+            + dot(weight_in[2], value_low)
+        )
+        input_grad_ref[block * PAIRS : (block + 1) * PAIRS, :] = pairs_of(input_grad)
+
+
+def attention_backward(
+    segment_ids, keep_mask, turned, joined, context, logsums, upstream, first_back, weight, codes
+):
+    every, width, unused = turned.shape
+    heads = width // HEAD_DIM
+    blocks = LEN // BLOCK
+    sequences = every // blocks
+
+    def whole(*shape):
+        return pl.BlockSpec(shape, lambda i, *refs: (0,) * len(shape))
+
+    def part(*shape):
+        return pl.BlockSpec(shape, lambda i, *refs: (i,) + (0,) * (len(shape) - 1))
+
+    return pl.pallas_call(
+        backward_kernel,
+        out_shape=(
+            jax.ShapeDtypeStruct((sequences * LEN // 2, 2 * width), F32),
+            jax.ShapeDtypeStruct((3, width, width), F32),
+            jax.ShapeDtypeStruct((2, width, 128), F32),
+        ),
+        grid_spec=pltpu.PrefetchScalarGridSpec(
+            num_scalar_prefetch=2,
+            grid=(sequences,),
+            in_specs=[
+                part(blocks, width, BLOCK),
+                part(blocks, 3, width, BLOCK),
+                part(blocks, width, BLOCK),
+                part(blocks, 8, BLOCK),
+                part(blocks, width, BLOCK),
+                part(blocks, width, BLOCK),
+                whole(3, width, width),
+                part(blocks, 8, BLOCK),
+            ],
+            out_specs=(
+                part(LEN // 2, 2 * width),
+                whole(3, width, width),
+                whole(2, width, 128),
+            ),
+            scratch_shapes=[
+                pltpu.VMEM((LEN, 128), F32),
+                pltpu.VMEM((heads, blocks, BLOCK, HEAD_DIM), BF16),
+                pltpu.VMEM((heads, blocks, BLOCK, HEAD_DIM), BF16),
+                pltpu.VMEM((blocks, width, BLOCK), BF16),
+                pltpu.VMEM((blocks, 8, BLOCK), F32),
+                pltpu.VMEM((blocks, width, BLOCK), F32),
+                pltpu.VMEM((blocks, width, BLOCK), F32),
+                pltpu.VMEM((blocks, width, BLOCK), F32),
+                pltpu.VMEM((3, width, width), BF16),
+            ],
+        ),
+        compiler_params=pltpu.CompilerParams(vmem_limit_bytes=VMEM_BYTES),
+        name="attention_backward",
+    )(segment_ids, keep_mask, turned, joined, context, logsums, upstream, first_back, weight, codes)
 
 
 def as_rows(paired):
@@ -53,123 +368,14 @@
     return (back, jnp.sum(upstream * normal, axis=0), jnp.sum(upstream, axis=0))
 
 
-def allowed_mask(segment_rows, keep_rows, offset, block_rows):
-    block_segment = segment_rows[offset : offset + block_rows]
-    query_places = offset + jnp.arange(block_rows, dtype=jnp.int32)
-    key_places = jnp.arange(segment_rows.shape[0], dtype=jnp.int32)
-    same_segment = block_segment[:, None] == segment_rows[None, :]
-    return same_segment & (
-        (keep_rows[None, :] == 1) | (query_places[:, None] == key_places[None, :])
-    )
-
-
-def block_scores(block_queries, key_rows, allowed):
-    raw_scores = jnp.einsum(
-        "qhd,khd->hqk", block_queries, key_rows, preferred_element_type=jnp.float32
-    ) * HEAD_DIM ** (-0.5)
-    return jnp.where(allowed[None], raw_scores, NEGATIVE)
-
-
-def attention_forward(queries, key_rows, value_rows, segment_ids, keep_mask):
-    row_count, channels = queries.shape
-    sequences = row_count // LEN
-    head_count = channels // HEAD_DIM
-    block_rows = min(512, LEN)
-    layout = (sequences, LEN, head_count, HEAD_DIM)
-
-    def per_sequence(state_carry, sequence_item):
-        seq_queries, seq_keys, seq_values, seq_segment, seq_keep = sequence_item
-        outputs = []
-        logsums = []
-        for block_index in range(LEN // block_rows):
-            offset = block_index * block_rows
-            allowed = allowed_mask(seq_segment, seq_keep, offset, block_rows)
-            scores = block_scores(seq_queries[offset : offset + block_rows], seq_keys, allowed)
-            highest = jnp.max(scores, axis=-1, keepdims=True)
-            exponent = jnp.exp(scores - highest)
-            totals = jnp.sum(exponent, axis=-1, keepdims=True)
-            weights = (exponent / totals).astype(jnp.bfloat16)
-            outputs.append(
-                jnp.einsum("hqk,khd->qhd", weights, seq_values, preferred_element_type=jnp.float32)
-            )
-            logsums.append((highest + jnp.log(totals))[:, :, 0])
-        return (state_carry, (jnp.concatenate(outputs, axis=0), jnp.concatenate(logsums, axis=1)))
-
-    items = (
-        queries.reshape(layout),
-        key_rows.reshape(layout),
-        value_rows.reshape(layout),
-        segment_ids.reshape(sequences, LEN),
-        keep_mask.reshape(sequences, LEN),
-    )
-    unused, (context, logsums) = lax.scan(per_sequence, jnp.float32(0), items)
-    return (context.reshape(row_count, channels), logsums)
-
-
-def attention_backward(queries, key_rows, value_rows, segment_ids, keep_mask, logsums, upstream):
-    row_count, channels = queries.shape
-    sequences = row_count // LEN
-    head_count = channels // HEAD_DIM
-    block_rows = min(512, LEN)
-    layout = (sequences, LEN, head_count, HEAD_DIM)
-    score_scale = HEAD_DIM ** (-0.5)
-
-    def per_sequence(state_carry, sequence_item):
-        seq_queries, seq_keys, seq_values, seq_segment, seq_keep, seq_logsums, seq_upstream = (
-            sequence_item
-        )
-        key_grad = jnp.zeros(seq_keys.shape, jnp.float32)
-        value_grad = jnp.zeros(seq_values.shape, jnp.float32)
-        query_grads = []
-        for block_index in range(LEN // block_rows):
-            offset = block_index * block_rows
-            block_queries = seq_queries[offset : offset + block_rows]
-            block_upstream = seq_upstream[offset : offset + block_rows]
-            allowed = allowed_mask(seq_segment, seq_keep, offset, block_rows)
-            weights = jnp.exp(
-                block_scores(block_queries, seq_keys, allowed)
-                - seq_logsums[:, offset : offset + block_rows, None]
-            )
-            value_grad = value_grad + jnp.einsum(
-                "hqk,qhd->khd",
-                weights.astype(jnp.bfloat16),
-                block_upstream,
-                preferred_element_type=jnp.float32,
-            )
-            weight_grad = jnp.einsum(
-                "qhd,khd->hqk", block_upstream, seq_values, preferred_element_type=jnp.float32
-            )
-            score_grad = (
-                weights * (weight_grad - jnp.sum(weight_grad * weights, axis=-1, keepdims=True))
-            ).astype(jnp.bfloat16)
-            query_grads.append(
-                jnp.einsum("hqk,khd->qhd", score_grad, seq_keys, preferred_element_type=jnp.float32)
-                * score_scale
-            )
-            key_grad = (
-                key_grad
-                + jnp.einsum(
-                    "hqk,qhd->khd", score_grad, block_queries, preferred_element_type=jnp.float32
-                )
-                * score_scale
-            )
-        return (state_carry, (jnp.concatenate(query_grads, axis=0), key_grad, value_grad))
-
-    items = (
-        queries.reshape(layout),
-        key_rows.reshape(layout),
-        value_rows.reshape(layout),
-        segment_ids.reshape(sequences, LEN),
-        keep_mask.reshape(sequences, LEN),
-        logsums,
-        upstream.reshape(layout),
-    )
-    unused, (query_back, key_back, value_back) = lax.scan(per_sequence, jnp.float32(0), items)
-    return (
-        query_back.reshape(row_count, channels),
-        key_back.reshape(row_count, channels),
-        value_back.reshape(row_count, channels),
-    )
+def rows_of(blocked):
+    every, width, unused = blocked.shape
+    return blocked.reshape(every, width, 2, PAIRS).transpose(0, 3, 2, 1).reshape(every * BLOCK, width)
+
+
+def columns_from(rows):
+    every, width = rows.shape[0] // BLOCK, rows.shape[1]
+    return rows.reshape(every, PAIRS, 2, width).transpose(0, 3, 2, 1).reshape(every, width, BLOCK)
 
 
 def spread(vector, row_devices):
@@ -197,6 +403,7 @@
     second_shift,
     cotangent,
 ):
+    pairs = inputs[:, 0, :]
     inputs = as_rows(inputs)
     cotangent = as_rows(cotangent)
     query_full, key_full, value_full, output_full, expand_full, reduce_full = (
@@ -207,11 +414,14 @@
         lax.all_gather(expand_weight, "row", axis=1, tiled=True),
         lax.all_gather(reduce_weight, "row", axis=1, tiled=True),
     )
-    queries = (forward_product(inputs, query_full) + query_bias).astype(jnp.bfloat16)
-    key_rows = forward_product(inputs, key_full).astype(jnp.bfloat16)
-    value_rows = (forward_product(inputs, value_full) + value_bias).astype(jnp.bfloat16)
-    context, logsums = attention_forward(queries, key_rows, value_rows, segment_ids, keep_mask)
-    context = context.astype(jnp.bfloat16)
+    every = segment_ids.shape[0] // BLOCK
+    coded = jnp.stack([segment_ids, jnp.where(keep_mask == 1, segment_ids, -1)]).astype(F32)
+    coded = coded.reshape(2, every, PAIRS, 2).transpose(1, 0, 3, 2).reshape(every, 2, BLOCK)
+    codes = jnp.pad(coded, ((0, 0), (0, 6), (0, 0)))
+    weight = jnp.stack([query_full.T, key_full.T, value_full.T])
+    vectors = jnp.pad(jnp.stack([query_bias, value_bias]), ((0, 6), (0, 0)))
+    turned, joined, context_t, logsums = attention_forward(pairs, segment_ids, keep_mask, weight, vectors, codes)
+    context = rows_of(context_t)
     attended = lax.psum_scatter(
         forward_product(context, output_full).astype(jnp.bfloat16),
         "col",
@@ -250,29 +460,12 @@
     upstream_whole = lax.all_gather(attended_back, "col", axis=1, tiled=True)
     context_grad = product_transposed(upstream_whole, output_full)
     grad_output = product_over_rows(context, upstream_whole)
-    query_back, key_back, value_back = attention_backward(
-        queries,
-        key_rows,
-        value_rows,
-        segment_ids,
-        keep_mask,
-        logsums,
-        context_grad.astype(jnp.bfloat16),
-    )
-    query_low = query_back.astype(jnp.bfloat16)
-    key_low = key_back.astype(jnp.bfloat16)
-    value_low = value_back.astype(jnp.bfloat16)
-    bias_query = jnp.sum(query_low.astype(jnp.float32), axis=0)
-    bias_value = jnp.sum(value_low.astype(jnp.float32), axis=0)
-    grad_query = product_over_rows(inputs, query_low)
-    grad_key = product_over_rows(inputs, key_low)
-    grad_value = product_over_rows(inputs, value_low)
-    input_grad = (
-        first_back
-        + product_transposed(query_low, query_full)
-        + product_transposed(key_low, key_full)
-        + product_transposed(value_low, value_full)
-    )
+    input_grad, weight_grad, bias_grad = attention_backward(
+        segment_ids, keep_mask, turned, joined, context_t, logsums, columns_from(context_grad.astype(BF16)),
+        columns_from(first_back), weight, codes)
+    bias_query = jnp.sum(bias_grad[0], axis=1)
+    bias_value = jnp.sum(bias_grad[1], axis=1)
+    grad_query, grad_key, grad_value = weight_grad[0].T, weight_grad[1].T, weight_grad[2].T
     row_devices = lax.axis_size("row")
     scattered = (
         lax.psum_scatter(
@@ -367,7 +560,7 @@
     )
     return (
         as_pairs(result.astype(jnp.bfloat16)),
-        as_pairs(input_grad),
+        input_grad[:, None, :],
         summed[0],
         summed[6],
         summed[1],

time: 677 us -> 551 us (0.81)
  matrix products: 173 us -> 62.9 us
  Pallas kernels: 0 us -> 68.2 us
  other arithmetic: 77.8 us -> 31.9 us
  local copies, waits for them, and re-layouts: 83.8 us -> 66.2 us
  blocking collectives: 136 us -> 126 us
  waiting for transfers between devices: 179 us -> 171 us
    dot_general x42 -> x0, matrix products: 87.7 us -> none  [the longest x6 25.7 us: per_sequence(): jnp.einsum('qhd,khd->hqk', block_upstream, seq_values, preferred_element_...]
    pallas_call x0 -> x2, Pallas kernels: none -> 68.2 us  [the longest x1 42.5 us: attention_backward(): pl.pallas_call(backward_kernel, out_shape=(jax.ShapeDtypeStruct((sequence...]
    convert_element_type x3 -> x0, other arithmetic: 23.4 us -> none  [per_sequence(): score_grad = (weights * (weight_grad - jnp.sum(weight_grad * weights, axi...]
    reduce_scatter x1, waiting for transfers between devices: 2.85 us -> 22.6 us  [local(): lax.psum_scatter(grad_value.astype(jnp.bfloat16), 'row', scatter_dimensio...]
    reduce_scatter x1, waiting for transfers between devices: 22.6 us -> 7.5 us  [local(): lax.psum_scatter(grad_key.astype(jnp.bfloat16), 'row', scatter_dimension=...]
    while x70 -> x0, local copies, waits for them, and re-layouts: 13.1 us -> none  [the longest x3 6.82 us: attention_forward(): unused, (context, logsums) = lax.scan(per_sequence, jnp.float32(0), items)]
    dot_general x6 -> x3, matrix products: 30.2 us -> 18.1 us  [product_transposed(): lax.dot_general(left, right, (((1,), (1,)), ((), ())), preferred_element_...]
    reduce_sum x5 -> x1, other arithmetic: 11 us -> 0.15 us  [local(): bias_value = jnp.sum(bias_grad[1], axis=1)]
  transfers between devices with their start and end apart: 9 -> 9, of which waited for: 6 -> 5; matrix products, arithmetic and copies ran while one was open for 30% -> 16% of each run, Pallas kernels for 0% -> 8%
where the time goes in v1:
time: 551 us; the launch traced here: 542 us
  waiting for transfers between devices  171 us (31%)
  blocking collectives  126 us (23%)
  Pallas kernels  68.2 us (12%)
  local copies, waits for them, and re-layouts  66.2 us (12%)
  matrix products  62.9 us (11%)
  other arithmetic  31.9 us (6%)
  between operations  15 us (3%)
    all_gather x1, waiting for transfers between devices, local(): upstream_whole = lax.all_gather(attended_back, 'col', axis=1, tiled=True)  68.4 us
    reduce_scatter x1, waiting for transfers between devices, local(): lax.psum_scatter(forward_product(context, output_full).astype(jnp.bfloat1...  62 us
    pallas_call x1, Pallas kernels, attention_backward(): pl.pallas_call(backward_kernel, out_shape=(jax.ShapeDtypeStruct((sequence...  42.5 us
    psum x2, blocking collectives, norm_forward(): lax.psum((jnp.sum(summed, axis=1), jnp.sum(summed * summed, axis=1)), 'col')  34.7 us
    psum x2, blocking collectives, norm_backward(): lax.psum((jnp.sum(scaled, axis=1), jnp.sum(scaled * normal, axis=1)), 'col')  33.6 us
    dot_general x3, matrix products, forward_product(): return jnp.dot(left, right, preferred_element_type=jnp.float32)  31 us
    pallas_call x1, Pallas kernels, attention_forward(): pl.pallas_call(forward_kernel, out_shape=(jax.ShapeDtypeStruct((every, wi...  25.7 us
    reduce_scatter x1, waiting for transfers between devices, local(): lax.psum_scatter(grad_value.astype(jnp.bfloat16), 'row', scatter_dimensio...  22.6 us
  transfers between devices with their start and end apart: 9, of which 5 were waited for; matrix products, arithmetic and copies ran while one was open for 16% of the time, Pallas kernels for 8%

profile of v1, /device:TPU:0, one launch (start us, length us, event | category | flops | bytes accessed | tf_op | source)
XLA Modules:
  0.0 541.9 jit_solution(12788281801097929523)
XLA Ops:
  10.8 6.4 %all_gather.21 = bf16[192,192]{0,1:T(8,128)(2,1)S(1)} all-gather(bf16[192,48]{0,1:T(8,128)(2,1)S(1)} %copy-done.20), channel_id=1, replica_groups=mesh['dp'=2,'row'=4,'col'=4] {'row'}, dimensions={1}, use_global_device_ids=true | all-gather | bytes 92160 | tf_op jit(solution)/shard_map/all_gather | solution.py:410
  17.2 5.6 %all_gather.22 = bf16[192,192]{0,1:T(8,128)(2,1)S(1)} all-gather(bf16[192,48]{0,1:T(8,128)(2,1)S(1)} %copy-done.21), channel_id=1, replica_groups=mesh['dp'=2,'row'=4,'col'=4] {'row'}, dimensions={1}, use_global_device_ids=true | all-gather | bytes 92160 | tf_op jit(solution)/shard_map/all_gather | solution.py:411
  22.8 5.3 all_gather.23
  30.1 25.7 %attention_forward.1 = (bf16[12,192,256]{2,1,0:T(8,128)(2,1)}, bf16[12,3,192,256]{3,2,1,0:T(8,128)(2,1)}, bf16[12,192,256]{2,1,0:T(8,128)(2,1)}, f32[12,8,256]{2,1,0:T(8,128)}) custom-call(s32[3072]{0:T(1024)} %segment_ref.3, s32[3072]{0:T(1024)} %keep_ref.3, bf16[1536,384]{1,0:T(8,128)(2,1)} %bitcast.56, bf16[3,192,192]{2,1,0:T(8,128)(2,1)} %pad_maximum_fusion.weight_ref, ...), custom_call_target="tpu_custom_call" | custom-call | tf_op jit(solution)/shard_map/attention_forward/pallas_call | solution.py:159
  63.3 6.1 %all_gather.24 = bf16[192,768]{0,1:T(8,128)(2,1)S(1)} all-gather(bf16[192,192]{0,1:T(8,128)(2,1)S(1)} %copy.53), channel_id=1, replica_groups=mesh['dp'=2,'row'=4,'col'=4] {'row'}, dimensions={1}, use_global_device_ids=true | all-gather | bytes 368640 | tf_op jit(solution)/shard_map/all_gather | solution.py:413
  82.9 6.8 %all_gather.25 = bf16[192,768]{0,1:T(8,128)(2,1)S(1)} all-gather(bf16[192,192]{0,1:T(8,128)(2,1)} %copy.55), channel_id=1, replica_groups=mesh['dp'=2,'row'=4,'col'=4] {'row'}, dimensions={1}, use_global_device_ids=true | all-gather | bytes 368640 | tf_op jit(solution)/shard_map/all_gather | solution.py:414
  89.7 7.3 %all_gather.26 = bf16[768,192]{0,1:T(8,128)(2,1)} all-gather(bf16[768,48]{0,1:T(8,128)(2,1)} %param.33), channel_id=1, replica_groups=mesh['dp'=2,'row'=4,'col'=4] {'row'}, dimensions={1}, use_global_device_ids=true | all-gather | bytes 368640 | tf_op jit(solution)/shard_map/all_gather | solution.py:415
  97.0 62.0 %reduce-scatter.12.cloned.1.call-done = bf16[3072,192]{0,1:T(8,128)(2,1)} async-done(((bf16[3072,768]{0,1:T(8,128)(2,1)}), bf16[3072,192]{0,1:T(8,128)(2,1)}) %reduce-scatter.12.cloned.1.call-update) | async-done | bytes 1179664 | tf_op jit(solution)/shard_map/reduce_scatter | solution.py:425
  158.9 4.5 fusion.42
  163.5 18.5 %all-reduce.14 = (f32[3072]{0:T(1024)S(1)}, f32[3072]{0:T(1024)S(1)}) all-reduce(f32[3072]{0:T(1024)} %get-tuple-element.91, f32[3072]{0:T(1024)S(1)} %get-tuple-element.90), channel_id=1, replica_groups=mesh['dp'=2,'row'=4,'col'=4] {'col'}, use_global_device_ids=true, to_apply=%region_4.5 | all-reduce | flops 6144 | bytes 49152 | tf_op jit(solution)/shard_map/psum | solution.py:357
  182.1 24.2 %fusion.2 = (bf16[3072,768]{1,0:T(8,128)(2,1)S(1)}, f32[3072,768]{1,0:T(8,128)}) fusion(f32[768]{0:T(1024)} %param.32, bf16[192,768]{0,1:T(8,128)(2,1)S(1)} %all_gather.25, f32[3072,192]{0,1:T(8,128)} %get-tuple-element.130, f32[192]{0:T(256)} %param.30, f32[192]{0:T(256)} %param.29, f32[3072]{0:T(1024)S(1)} %get-tuple-element.138, ...), kind=kOutput, calls=%fused_computation.4 | convolution fusion | flops 1064632320 | bytes 16839168 | tf_op jit(solution)/shard_map/dot_general | solution.py:341
  209.6 16.2 %all-reduce.13 = (f32[3072]{0:T(1024)S(1)}, f32[3072]{0:T(1024)S(1)}) all-reduce(f32[3072]{0:T(1024)S(1)} %get-tuple-element.89, f32[3072]{0:T(1024)S(1)} %get-tuple-element.88), channel_id=1, replica_groups=mesh['dp'=2,'row'=4,'col'=4] {'col'}, use_global_device_ids=true, to_apply=%region_8.9 | all-reduce | flops 6144 | bytes 49152 | tf_op jit(solution)/shard_map/psum | solution.py:357
  228.1 17.4 %all-reduce.12 = (f32[3072]{0:T(1024)S(1)}, f32[3072]{0:T(1024)S(1)}) all-reduce(f32[3072]{0:T(1024)S(1)} %get-tuple-element.93, f32[3072]{0:T(1024)S(1)} %get-tuple-element.92), channel_id=1, replica_groups=mesh['dp'=2,'row'=4,'col'=4] {'col'}, use_global_device_ids=true, to_apply=%region_12.13 | all-reduce | flops 6144 | bytes 49152 | tf_op jit(solution)/shard_map/psum | solution.py:366
  245.7 8.7 %fusion.44 = (bf16[768]{0:T(1024)(128)(2,1)}, bf16[3072,768]{1,0:T(8,128)(2,1)S(1)}) fusion(f32[3072,768]{1,0:T(8,128)} %get-tuple-element.140, f32[768]{0:T(1024)S(1)} %copy-done.36, bf16[768,192]{0,1:T(8,128)(2,1)S(1)} %copy-done.9, f32[3072]{0:T(1024)S(1)} %get-tuple-element.98, f32[3072,192]{0,1:T(8,128)} %get-tuple-element.141, ...), kind=kOutput, calls=%fused_computation.95 | convolution fusion | flops 940178688 | bytes 18044160 | tf_op jit(solution)/shard_map/dot_general | solution.py:345
  254.5 4.9 multiply_reduce_fusion
  259.4 16.1 %all-reduce.11 = (f32[3072]{0:T(1024)S(1)}, f32[3072]{0:T(1024)S(1)}) all-reduce(f32[3072]{0:T(1024)S(1)} %get-tuple-element.83, f32[3072]{0:T(1024)S(1)} %get-tuple-element.86), channel_id=1, replica_groups=mesh['dp'=2,'row'=4,'col'=4] {'col'}, use_global_device_ids=true, to_apply=%region_16.17 | all-reduce | flops 6144 | bytes 49152 | tf_op jit(solution)/shard_map/psum | solution.py:366
  280.7 4.3 convolution_convert_fusion.3
  292.1 4.5 copy.61
  296.6 4.3 reshape.115.first_back_ref
  300.9 68.4 %all-gather.2.cloned.1.call-done = bf16[3072,768]{0,1:T(8,128)(2,1)} async-done(((bf16[3072,192]{0,1:T(8,128)(2,1)}), bf16[3072,768]{0,1:T(8,128)(2,1)}) %all-gather.2.cloned.1.call-update) | async-done | bytes 4718608 | tf_op jit(solution)/shard_map/all_gather | solution.py:460
  369.3 4.1 convolution_convert_fusion.4
  374.7 5.4 %convolution_convert_fusion.2 = bf16[768,192]{0,1:T(8,128)(2,1)} fusion(bf16[3072,768]{1,0:T(8,128)(2,1)} %copy-done.42, bf16[3072,192]{0,1:T(8,128)(2,1)S(1)} %copy-done.3, f32[3072,192]{0,1:T(8,128)} %get-tuple-element.141, f32[3072]{0:T(1024)S(1)} %copy-done.24, f32[3072]{0:T(1024)S(1)} %copy-done.15, f32[192]{0:T(256)S(1)} %copy-done.25, ...), kind=kOutput, calls=%fused_computation.51 | convolution fusion | flops 912015360 | bytes 8602368 | tf_op jit(solution)/shard_map/dot_general | solution.py:351
  380.2 4.5 convolution_convert_fusion.1
  388.4 5.3 copy.59
  395.3 42.5 %attention_backward.1 = (f32[1536,384]{1,0:T(8,128)}, f32[3,192,192]{2,1,0:T(8,128)}, f32[2,192,128]{2,1,0:T(8,128)}) custom-call(s32[3072]{0:T(1024)} %segment_ref.3, s32[3072]{0:T(1024)} %keep_ref.3, bf16[12,192,256]{2,1,0:T(8,128)(2,1)} %get-tuple-element.25.turned_ref, bf16[12,3,192,256]{3,2,1,0:T(8,128)(2,1)} %get-tuple-element.26.joined_ref, ...), custom_call_target="tpu_custom_call" | custom-call | tf_op jit(solution)/shard_map/attention_backward/pallas_call | solution.py:290
  445.7 4.3 fusion.22
  453.6 6.5 %copy.62 = f32[1536,1,384]{2,1,0:T(1,128)} copy(f32[1536,1,384]{2,0,1:T(8,128)} %bitcast.57) | data formatting | bytes 4718592
  460.4 10.3 %all-reduce.15 = (bf16[192,4]{0,1:T(4,128)(2,1)S(1)}, bf16[192,4]{0,1:T(4,128)(2,1)S(1)}, bf16[192,4]{0,1:T(4,128)(2,1)S(1)}, bf16[192,4]{0,1:T(4,128)(2,1)S(1)}...) all-reduce(bf16[192,4]{0,1:T(4,128)(2,1)S(1)} %broadcast_in_dim.26,, ...), channel_id=4, replica_groups=mesh['dp'=2,'row'=4,'col'=4] {'row'}, use_global_device_ids=true, to_apply=%region_20.21.clone | all-reduce | flops 9216 | bytes 36864
  474.0 7.5 %reduce-scatter.16.cloned.1.call-done = bf16[192,48]{0,1:T(8,128)(2,1)} async-done(((bf16[192,192]{0,1:T(8,128)(2,1)}), bf16[192,48]{0,1:T(8,128)(2,1)}) %reduce-scatter.16.cloned.1.call-update) | async-done | bytes 18448 | tf_op jit(solution)/shard_map/reduce_scatter | solution.py:474
  481.5 22.6 %reduce-scatter.18.cloned.1.call-done = bf16[192,48]{0,1:T(8,128)(2,1)} async-done(((bf16[192,192]{0,1:T(8,128)(2,1)}), bf16[192,48]{0,1:T(8,128)(2,1)}) %reduce-scatter.18.cloned.1.call-update) | async-done | bytes 18448 | tf_op jit(solution)/shard_map/reduce_scatter | solution.py:477
  504.2 10.3 %all-reduce.16 = (bf16[192,48]{0,1:T(8,128)(2,1)S(1)}, bf16[192]{0:T(256)(128)(2,1)S(1)}, bf16[192,48]{0,1:T(8,128)(2,1)S(1)}, bf16[192,48]{0,1:T(8,128)(2,1)S(1...) all-reduce(bf16[192,48]{0,1:T(8,128)(2,1)} %reduce-scatter.14.clone, ...), channel_id=1, replica_groups=mesh['dp'=2,'row'=4,'col'=4] {'dp'}, use_global_device_ids=true, to_apply=%region_18.19 | all-reduce | flops 29952 | bytes 119808 | tf_op jit(solution)/shard_map/psum | solution.py:545
  521.4 8.8 %all-reduce.20.cloned.1.call-done = (bf16[192,192]{1,0:T(8,128)(2,1)}, bf16[192,192]{1,0:T(8,128)(2,1)}, bf16[768,48]{0,1:T(8,128)(2,1)}) async-done(((bf16[192,192]{1,0:T(8,128)(2,1)}, bf16[192,192]{1,0:T(8,128)(2,1)}, bf16[768,48]{0,1:T(8,128)(2,1)}), (bf16[192,192]{1,0:T(8,128)(2,1)}, bf16[192,192]{1,0:T(8,128)(2,1)}, bf16[768,48]{0,1:T(8,128)(2,1)})) %all-reduce.20.cloned.1.call-update) | async-done | bytes 221200 | tf_op jit(solution)/shard_map/psum | solution.py:548
  (182 shorter events, 77.5 us)
Async XLA Ops:
  7.2 10.0 %copy-start.21 = (bf16[192,48]{0,1:T(8,128)(2,1)S(1)}, bf16[192,48]{0,1:T(8,128)(2,1)}, u32[]{:S(2)}) copy-start(bf16[192,48]{0,1:T(8,128)(2,1)} %param.24) | copy-start | bytes 55300
  7.2 15.6 %copy-start.22 = (bf16[192,48]{0,1:T(8,128)(2,1)S(1)}, bf16[192,48]{0,1:T(8,128)(2,1)}, u32[]{:S(2)}) copy-start(bf16[192,48]{0,1:T(8,128)(2,1)} %param.25) | copy-start | bytes 55300
  7.2 21.5 %copy-start.31 = (f32[192]{0:T(256)S(1)}, f32[192]{0:T(256)}, u32[]{:S(2)}) copy-start(f32[192]{0:T(256)} %param.23) | copy-start | bytes 2308
  7.2 21.5 %copy-start.30 = (f32[192]{0:T(256)S(1)}, f32[192]{0:T(256)}, u32[]{:S(2)}) copy-start(f32[192]{0:T(256)} %param.26) | copy-start | bytes 2308
  7.2 151.7 %reduce-scatter.12.cloned.1.call-start = ((), (), s32[]{:S(2)}) async-start(), calls=%async_computation.7 | async-start | bytes 5898240 | tf_op jit(solution)/shard_map/reduce_scatter | solution.py:425
  63.2 9.8 %copy-start.7 = (bf16[3072,192]{1,0:T(8,128)(2,1)}, bf16[3072,192]{1,0:T(8,128)(2,1)S(1)}, u32[]{:S(2)}) copy-start(bf16[3072,192]{1,0:T(8,128)(2,1)S(1)} %reshape.109) | copy-start | bytes 3538948
  73.1 296.2 %all-gather.2.cloned.1.call-start = ((), (), s32[]{:S(2)}) async-start(), calls=%async_computation.8 | async-start | bytes 5898240 | tf_op jit(solution)/shard_map/all_gather | solution.py:460
  82.2 81.2 %copy-start = (bf16[3072,192]{1,0:T(8,128)(2,1)}, bf16[3072,192]{1,0:T(8,128)(2,1)S(1)}, u32[]{:S(2)}) copy-start(bf16[3072,192]{1,0:T(8,128)(2,1)S(1)} %reshape.111) | copy-start | bytes 3538948
  82.2 76.7 %copy-start.28 = (f32[192]{0:T(256)S(1)}, f32[192]{0:T(256)}, u32[]{:S(2)}) copy-start(f32[192]{0:T(256)} %param.28) | copy-start | bytes 2308
  82.9 171.5 %copy-start.2 = (bf16[3072,192]{0,1:T(8,128)(2,1)}, bf16[3072,192]{0,1:T(8,128)(2,1)S(1)}, u32[]{:S(2)}) copy-start(bf16[3072,192]{0,1:T(8,128)(2,1)S(1)} %copy.57) | copy-start | bytes 3538948
  182.0 72.4 %copy-start.16 = (f32[3072]{0:T(1024)}, f32[3072]{0:T(1024)S(1)}, u32[]{:S(2)}) copy-start(f32[3072]{0:T(1024)S(1)} %get-tuple-element.137) | copy-start | bytes 36868
  182.0 72.4 %copy-start.18 = (f32[3072]{0:T(1024)}, f32[3072]{0:T(1024)S(1)}, u32[]{:S(2)}) copy-start(f32[3072]{0:T(1024)S(1)} %get-tuple-element.138) | copy-start | bytes 36868
  182.1 24.3 %copy-start.5 = (f32[3072,192]{0,1:T(8,128)S(1)}, f32[3072,192]{0,1:T(8,128)}, u32[]{:S(2)}) copy-start(f32[3072,192]{0,1:T(8,128)} %get-tuple-element.130) | copy-start | bytes 7077892
  182.1 24.3 %copy-start.9 = (bf16[768,192]{0,1:T(8,128)(2,1)S(1)}, bf16[768,192]{0,1:T(8,128)(2,1)}, u32[]{:S(2)}) copy-start(bf16[768,192]{0,1:T(8,128)(2,1)} %all_gather.26) | copy-start | bytes 884740
  182.1 24.3 %copy-start.32 = (f32[192]{0:T(256)S(1)}, f32[192]{0:T(256)}, u32[]{:S(2)}) copy-start(f32[192]{0:T(256)} %param.29) | copy-start | bytes 2308
  182.1 24.3 %copy-start.37 = (f32[192]{0:T(256)S(1)}, f32[192]{0:T(256)}, u32[]{:S(2)}) copy-start(f32[192]{0:T(256)} %param.34) | copy-start | bytes 2308
  182.1 24.3 %copy-start.38 = (f32[192]{0:T(256)S(1)}, f32[192]{0:T(256)}, u32[]{:S(2)}) copy-start(f32[192]{0:T(256)} %param.30) | copy-start | bytes 2308
  206.4 19.5 %copy-start.25 = (f32[192]{0:T(256)S(1)}, f32[192]{0:T(256)}, u32[]{:S(2)}) copy-start(f32[192]{0:T(256)} %param.35) | copy-start | bytes 2308
  209.6 36.0 %copy-start.36 = (f32[768]{0:T(1024)S(1)}, f32[768]{0:T(1024)}, u32[]{:S(2)}) copy-start(f32[768]{0:T(1024)} %param.32) | copy-start | bytes 9220
  225.8 28.6 %copy-start.11 = (f32[3072]{0:T(1024)}, f32[3072]{0:T(1024)S(1)}, u32[]{:S(2)}) copy-start(f32[3072]{0:T(1024)S(1)} %get-tuple-element.136) | copy-start | bytes 36868
  280.6 161.8 %reduce-scatter.24.cloned.1.call-start = ((), (), s32[]{:S(2)}) async-start(), calls=%async_computation.14 | async-start | bytes 491520
  285.9 158.2 %reduce-scatter.22.cloned.1.call-start = ((), (), s32[]{:S(2)}) async-start(), calls=%async_computation.13 | async-start | bytes 491520
  296.6 72.7 %copy-start.8 = (bf16[3072,192]{1,0:T(8,128)(2,1)S(1)}, bf16[3072,192]{1,0:T(8,128)(2,1)}, u32[]{:S(2)}) copy-start(bf16[3072,192]{1,0:T(8,128)(2,1)} %copy-done.7) | copy-start | bytes 3538948
  300.9 73.8 %copy-start.3 = (bf16[3072,192]{0,1:T(8,128)(2,1)S(1)}, bf16[3072,192]{0,1:T(8,128)(2,1)}, u32[]{:S(2)}) copy-start(bf16[3072,192]{0,1:T(8,128)(2,1)} %copy-done.2) | copy-start | bytes 3538948
  300.9 73.8 %copy-start.12 = (f32[3072]{0:T(1024)S(1)}, f32[3072]{0:T(1024)}, u32[]{:S(2)}) copy-start(f32[3072]{0:T(1024)} %copy-done.11) | copy-start | bytes 36868
  300.9 73.8 %copy-start.15 = (f32[3072]{0:T(1024)S(1)}, f32[3072]{0:T(1024)}, u32[]{:S(2)}) copy-start(f32[3072]{0:T(1024)} %copy-done.14) | copy-start | bytes 36868
  300.9 73.8 %copy-start.24 = (f32[3072]{0:T(1024)S(1)}, f32[3072]{0:T(1024)}, u32[]{:S(2)}) copy-start(f32[3072]{0:T(1024)} %copy-done.23) | copy-start | bytes 36868
  374.3 71.4 %reduce-scatter.20.cloned.1.call-start = ((), (), s32[]{:S(2)}) async-start(), calls=%async_computation.12 | async-start | bytes 368640 | tf_op jit(solution)/shard_map/reduce_scatter | solution.py:486
  380.1 93.9 %reduce-scatter.14.cloned.1.call-start = ((), (), s32[]{:S(2)}) async-start(), calls=%async_computation.9 | async-start | bytes 122880 | tf_op jit(solution)/shard_map/reduce_scatter | solution.py:471
  439.8 41.7 %reduce-scatter.16.cloned.1.call-start = ((), (), s32[]{:S(2)}) async-start(), calls=%async_computation.10 | async-start | bytes 122880 | tf_op jit(solution)/shard_map/reduce_scatter | solution.py:474
  440.6 63.6 %reduce-scatter.18.cloned.1.call-start = ((), (), s32[]{:S(2)}) async-start(), calls=%async_computation.11 | async-start | bytes 122880 | tf_op jit(solution)/shard_map/reduce_scatter | solution.py:477
  441.3 88.9 %all-reduce.20.cloned.1.call-start = ((), (), s32[]{:S(2)}) async-start(), calls=%async_computation.15 | async-start | bytes 540672 | tf_op jit(solution)/shard_map/psum | solution.py:548
  (20 other events, 106.0 us)
Sparse Core Ops, SparseCore 0:
  73.2 85.7 reduce-scatter.11
  280.7 88.5 all-gather.1
  371.8 19.2 reduce-scatter.23
  393.4 20.8 reduce-scatter.21
  416.6 20.2 reduce-scatter.19
  439.9 18.8 reduce-scatter.13
  461.8 19.6 reduce-scatter.15
  484.5 19.6 reduce-scatter.17
  506.6 23.5 all-reduce.19

commit v2 on v1

--- a/solution.py
+++ b/solution.py
@@ -329,300 +329,726 @@
     )(segment_ids, keep_mask, turned, joined, context, logsums, upstream, first_back, weight, codes)
 
 
-def as_rows(paired):
-    return paired.reshape(paired.shape[0] * 2, paired.shape[2] // 2)
-
-
-def as_pairs(matrix):
-    return matrix.reshape(matrix.shape[0] // 2, 1, matrix.shape[1] * 2)
-
-
-def forward_product(left, right):
-    return jnp.dot(left, right, preferred_element_type=jnp.float32)
-
-
-def product_transposed(left, right):
-    return lax.dot_general(
-        left, right, (((1,), (1,)), ((), ())), preferred_element_type=jnp.float32
+def peer_of(axis, size, distance):
+    return lax.rem(lax.axis_index(axis) + distance, size)
+
+
+def source_of(axis, size, distance):
+    return lax.rem(lax.axis_index(axis) + size - distance, size)
+
+
+def greet(axes):
+    barrier = pltpu.get_barrier_semaphore()
+    count = 0
+    for axis, size in axes:
+        for distance in range(1, size):
+            pl.semaphore_signal(
+                barrier, inc=1, device_id={axis: peer_of(axis, size, distance)}, device_id_type=MESH
+            )
+            count += 1
+    pl.semaphore_wait(barrier, count)
+
+
+def remote(source, target, send_sem, recv_sem, axis, peer):
+    return pltpu.make_async_remote_copy(
+        src_ref=source, dst_ref=target, send_sem=send_sem, recv_sem=recv_sem,
+        device_id={axis: peer}, device_id_type=MESH,
     )
 
 
-def product_over_rows(left, right):
-    return lax.dot_general(
-        left, right, (((0,), (0,)), ((), ())), preferred_element_type=jnp.float32
-    )
-
-
-def norm_forward(summed, norm_gain, norm_shift):
-    totals = lax.psum((jnp.sum(summed, axis=1), jnp.sum(summed * summed, axis=1)), "col")
-    center = totals[0] / D
-    inverse = lax.rsqrt(totals[1] / D - center * center + EPSILON)
-    normal = (summed - center[:, None]) * inverse[:, None]
-    return (normal * norm_gain + norm_shift, normal, inverse)
-
-
-def norm_backward(upstream, normal, inverse, norm_gain):
-    scaled = upstream * norm_gain
-    totals = lax.psum((jnp.sum(scaled, axis=1), jnp.sum(scaled * normal, axis=1)), "col")
-    back = inverse[:, None] * (scaled - totals[0][:, None] / D - normal * totals[1][:, None] / D)
-    return (back, jnp.sum(upstream * normal, axis=0), jnp.sum(upstream, axis=0))
-
-
-def rows_of(blocked):
-    every, width, unused = blocked.shape
-    return blocked.reshape(every, width, 2, PAIRS).transpose(0, 3, 2, 1).reshape(every * BLOCK, width)
-
-
-def columns_from(rows):
-    every, width = rows.shape[0] // BLOCK, rows.shape[1]
-    return rows.reshape(every, PAIRS, 2, width).transpose(0, 3, 2, 1).reshape(every, width, BLOCK)
-
-
-def spread(vector, row_devices):
-    return jnp.broadcast_to(vector[:, None], (vector.shape[0], row_devices))
+def gather_kernel(rows, cols, query_ref, key_ref, value_ref, output_ref, joined_ref, output_all_ref, send, recv):
+    row, col = lax.axis_index("row"), lax.axis_index("col")
+    greet((("row", rows), ("col", cols)))
+    copies = []
+    for distance in range(1, rows):
+        peer = peer_of("row", rows, distance)
+        for kind, ref in enumerate((query_ref, key_ref, value_ref)):
+            place = (kind, distance - 1)
+            copies.append(remote(ref, joined_ref.at[kind, row], send.at[place], recv.at[place], "row", peer))
+    for distance in range(1, cols):
+        peer = peer_of("col", cols, distance)
+        place = (3, distance - 1)
+        copies.append(remote(output_ref, output_all_ref.at[col], send.at[place], recv.at[place], "col", peer))
+    for copy in copies:
+        copy.start()
+    for kind, ref in enumerate((query_ref, key_ref, value_ref)):
+        joined_ref[kind, row] = ref[...]
+    output_all_ref[col] = output_ref[...]
+    for copy in copies:
+        copy.wait()
+
+
+def gather_weights(rows, cols, query, key, value, output):
+    part, width = query.shape
+    return pl.pallas_call(
+        functools.partial(gather_kernel, rows, cols),
+        out_shape=(
+            jax.ShapeDtypeStruct((3, rows, part, width), BF16),
+            jax.ShapeDtypeStruct((cols,) + output.shape, BF16),
+        ),
+        in_specs=[vmem_spec()] * 4,
+        out_specs=(vmem_spec(), vmem_spec()),
+        scratch_shapes=[
+            pltpu.SemaphoreType.DMA((4, max(rows, cols) - 1)),
+            pltpu.SemaphoreType.DMA((4, max(rows, cols) - 1)),
+        ],
+        compiler_params=pltpu.CompilerParams(collective_id=0, has_side_effects=True),
+        name="gather_weights",
+    )(query, key, value, output)
+
+
+ROWS = 32
+QUERY_BIAS, VALUE_BIAS, OUTPUT_BIAS, FIRST_GAIN, FIRST_SHIFT, REDUCE_BIAS, SECOND_GAIN, SECOND_SHIFT, EXPAND_BIAS = range(9)
+GAIN_SECOND, SHIFT_SECOND, BIAS_REDUCE, GAIN_FIRST, SHIFT_FIRST, BIAS_OUTPUT, BIAS_EXPAND = range(7)
+
+
+def fold(value):
+    return jnp.sum(value.reshape(value.shape[0] // 8, 8, value.shape[1]), axis=0)
+
+
+def halves(value):
+    return value[:, :128] + value[:, 128:]
+
+
+def middle_kernel(
+    rows, cols,
+    turned_ref, context_ref, cotangent_ref, output_weight_ref, expand_weight_ref, reduce_weight_ref, vectors_ref,
+    result_ref, first_back_ref, context_back_ref, grad_output_ref, grad_expand_ref, grad_reduce_ref, sums_ref,
+    contexts, attended_out, attended_in, backs_out, backs_in, context_back_out,
+    stat_out, stat_in, wide_out, wide_in, back_out, back_in,
+    output_parts, expand_parts, reduce_parts,
+    output_natural, output_turned, expand_natural, expand_turned, reduce_natural, reduce_turned,
+    columns, first_sum, second_sum, middle_low, first_inverse, hidden, activated, slope,
+    hidden_back, narrow, low_rows, cotangents,
+    weight_send, weight_recv, send, recv,
+):
+    row, me = lax.axis_index("row"), lax.axis_index("col")
+    width = turned_ref.shape[1]
+    blocks = LEN // BLOCK
+    chunks = turned_ref.shape[0] // blocks
+    greet((("row", rows), ("col", cols)))
+
+    kinds = ("contexts", "attended", "first", "second", "third", "backs", "context_back")
+
+    def transfers(kind, chunk):
+        made = []
+        for distance in range(1, cols):
+            peer = peer_of("col", cols, distance)
+            place = (kinds.index(kind), chunk, distance - 1)
+            if kind == "contexts":
+                source, target = context_ref.at[chunk * blocks + peer], contexts.at[chunk, me]
+            elif kind == "attended":
+                source, target = attended_out.at[chunk, peer], attended_in.at[chunk, me]
+            elif kind == "first":
+                source, target = stat_out.at[chunk], stat_in.at[chunk, me]
+            elif kind == "second":
+                source, target = wide_out.at[chunk], wide_in.at[chunk, me]
+            elif kind == "third":
+                source, target = back_out.at[chunk], back_in.at[chunk, me]
+            elif kind == "backs":
+                source, target = backs_out.at[chunk * blocks + peer], backs_in.at[chunk, me]
+            else:
+                source, target = context_back_out.at[chunk, peer], context_back_ref.at[chunk * blocks + me]
+            made.append(remote(source, target, send.at[place], recv.at[place], "col", peer))
+        return made
+
+    def begin(kind, chunk):
+        for copy in transfers(kind, chunk):
+            copy.start()
+
+    def arrive(kind, chunk):
+        for copy in transfers(kind, chunk):
+            copy.wait_recv()
+
+    for chunk in range(chunks):
+        begin("contexts", chunk)
+    weights = []
+    for distance in range(1, rows):
+        peer = peer_of("row", rows, distance)
+        for kind, (source, target) in enumerate(
+            ((output_weight_ref, output_parts), (expand_weight_ref, expand_parts), (reduce_weight_ref, reduce_parts))
+        ):
+            place = (kind, distance - 1)
+            weights.append(
+                remote(source, target.at[row], weight_send.at[place], weight_recv.at[place], "row", peer)
+            )
+    for kind in range(3):
+        for copy in weights[kind::3]:
+            copy.start()
+    output_parts[row] = output_weight_ref[...]
+    expand_parts[row] = expand_weight_ref[...]
+    reduce_parts[row] = reduce_weight_ref[...]
+
+    turned_vectors = vectors_ref[...].T
+    for kind in range(columns.shape[0]):
+        columns[kind] = jnp.broadcast_to(turned_vectors[:, kind : kind + 1], (width, 128))
+    sums_ref[...] = jnp.zeros_like(sums_ref)
+    grad_expand_ref[...] = jnp.zeros_like(grad_expand_ref)
+    grad_reduce_ref[...] = jnp.zeros_like(grad_reduce_ref)
+    for chunk in range(chunks):
+        contexts[chunk, me] = context_ref[chunk * blocks + me]
+
+    def turn_cotangent(block, carry):
+        start = pl.multiple_of(block * PAIRS, PAIRS)
+        cotangents[block] = columns_of(cotangent_ref[pl.ds(start, PAIRS), :])
+        return carry
+
+    lax.fori_loop(0, chunks * blocks, turn_cotangent, 0)
+
+    def column(kind, at):
+        part = columns[kind, pl.ds(at, ROWS), :]
+        return jnp.concatenate([part, part], axis=1)
+
+    def over_rows(count, body, carry):
+        def step(index, carry):
+            return body(pl.multiple_of(index * ROWS, ROWS), carry)
+
+        return lax.fori_loop(0, count // ROWS, step, carry)
+
+    def total(value):
+        return jnp.sum(value, axis=0, keepdims=True)
+
+    def add_sum(kind, at, value):
+        sums_ref[kind, pl.ds(at, ROWS), :] += halves(value)
+
+    def over_blocks(chunk, body):
+        def step(block, carry):
+            body(block, chunk * blocks + block)
+            return carry
+
+        lax.fori_loop(0, blocks, step, 0)
+
+    zero = jnp.zeros((8, BLOCK), F32)
+
+    def project(chunk):
+        arrive("contexts", chunk)
+        attended = dot(output_turned[...], contexts[chunk].reshape(cols * width, BLOCK))
+        for group in range(cols):
+            attended_out[chunk, group] = attended[group * width : (group + 1) * width].astype(BF16)
+        begin("attended", chunk)
+        attended_in[chunk, me] = attended_out[chunk, me]
+
+    def add_first(chunk):
+        arrive("attended", chunk)
+
+        def body(block, place):
+            def part(at, carry):
+                here = pl.ds(at, ROWS)
+                summed = (
+                    turned_ref[place, here, :].astype(F32)
+                    + attended_in[chunk, block, here, :].astype(F32)
+                    + column(OUTPUT_BIAS, at)
+                )
+                first_sum[place, here, :] = summed
+                return carry[0] + fold(summed), carry[1] + fold(summed * summed)
+
+            one, two = over_rows(width, part, (zero, zero))
+            stat_out[chunk, pl.ds(2 * block, 1), :] = total(one)
+            stat_out[chunk, pl.ds(2 * block + 1, 1), :] = total(two)
+
+        over_blocks(chunk, body)
+        begin("first", chunk)
+
+    def gathered(own, others, chunk, index):
+        summed = jnp.zeros((1, BLOCK), F32)
+        for source in range(cols):
+            summed += others[chunk, source, pl.ds(index, 1), :]
+        return summed
+
+    def feed_forward(chunk):
+        arrive("first", chunk)
+        stat_in[chunk, me] = stat_out[chunk]
+
+        def body(block, place):
+            center = gathered(stat_out, stat_in, chunk, 2 * block) / D
+            inverse = lax.rsqrt(
+                gathered(stat_out, stat_in, chunk, 2 * block + 1) / D - center * center + EPSILON
+            )
+            first_inverse[place] = inverse
+
+            def normalize(at, carry):
+                here = pl.ds(at, ROWS)
+                normal = (first_sum[place, here, :] - center) * inverse
+                first_sum[place, here, :] = normal
+                middle_low[place, here, :] = (
+                    normal * column(FIRST_GAIN, at) + column(FIRST_SHIFT, at)
+                ).astype(BF16)
+                return carry
+
+            over_rows(width, normalize, 0)
+            hidden[...] = dot(expand_turned[...], middle_low[place])
+            for quarter in range(hidden.shape[0] // width):
+
+                def gelu(at, carry):
+                    here = pl.ds(quarter * width + at, ROWS)
+                    value = hidden[here, :] + column(EXPAND_BIAS + quarter, at)
+                    share = 0.5 * (1.0 + lax.erf(value * ROOT_HALF))
+                    activated[place, here, :] = (value * share).astype(BF16)
+                    slope[place, here, :] = share + value * DENSITY_SCALE * jnp.exp(-0.5 * value * value)
+                    return carry
+
+                over_rows(width, gelu, 0)
+            narrow[...] = dot(reduce_turned[...], activated[place])
+
+            def add_second(at, carry):
+                here = pl.ds(at, ROWS)
+                middle = first_sum[place, here, :] * column(FIRST_GAIN, at) + column(FIRST_SHIFT, at)
+                summed = middle + narrow[here, :] + column(REDUCE_BIAS, at)
+                second_sum[place, here, :] = summed
+                scaled = cotangents[place, here, :].astype(F32) * column(SECOND_GAIN, at)
+                return (
+                    carry[0] + fold(summed),
+                    carry[1] + fold(summed * summed),
+                    carry[2] + fold(scaled),
+                    carry[3] + fold(scaled * summed),
+                )
+
+            found = over_rows(width, add_second, (zero,) * 4)
+            for kind in range(4):
+                wide_out[chunk, pl.ds(4 * block + kind, 1), :] = total(found[kind])
+
+        over_blocks(chunk, body)
+        begin("second", chunk)
+
+    def feed_back(chunk):
+        arrive("second", chunk)
+        wide_in[chunk, me] = wide_out[chunk]
+
+        def body(block, place):
+            found = [gathered(wide_out, wide_in, chunk, 4 * block + kind) for kind in range(4)]
+            center = found[0] / D
+            inverse = lax.rsqrt(found[1] / D - center * center + EPSILON)
+            mean_scaled = found[2] / D
+            mean_product = inverse * (found[3] - center * found[2]) / D
+
+            def back_norm(at, carry):
+                here = pl.ds(at, ROWS)
+                normal = (second_sum[place, here, :] - center) * inverse
+                upstream = cotangents[place, here, :].astype(F32)
+                gain = column(SECOND_GAIN, at)
+                low_rows[here, :] = (normal * gain + column(SECOND_SHIFT, at)).astype(BF16)
+                back = inverse * (upstream * gain - mean_scaled - normal * mean_product)
+                second_sum[place, here, :] = back
+                add_sum(GAIN_SECOND, at, upstream * normal)
+                add_sum(SHIFT_SECOND, at, upstream)
+                add_sum(BIAS_REDUCE, at, back)
+                return carry
+
+            over_rows(width, back_norm, 0)
+            start = pl.multiple_of(place * PAIRS, PAIRS)
+            result_ref[pl.ds(start, PAIRS), :] = pairs_of(low_rows[...])
+            back_low = second_sum[place].astype(BF16)
+            hidden[...] = dot(reduce_natural[...], back_low)
+            for quarter in range(hidden.shape[0] // width):
+
+                def back_gelu(at, carry):
+                    here = pl.ds(quarter * width + at, ROWS)
+                    back = (hidden[here, :] * slope[place, here, :]).astype(BF16)
+                    hidden_back[here, :] = back
+                    add_sum(BIAS_EXPAND + quarter, at, back.astype(F32))
+                    return carry
+
+                over_rows(width, back_gelu, 0)
+            grad_reduce_ref[...] += dot_nt(back_low, activated[place])
+            grad_expand_ref[...] += dot_nt(hidden_back[...], middle_low[place])
+            narrow[...] = dot(expand_natural[...], hidden_back[...])
+
+            def add_middle(at, carry):
+                here = pl.ds(at, ROWS)
+                back = second_sum[place, here, :] + narrow[here, :]
+                second_sum[place, here, :] = back
+                normal = first_sum[place, here, :]
+                add_sum(GAIN_FIRST, at, back * normal)
+                add_sum(SHIFT_FIRST, at, back)
+                scaled = back * column(FIRST_GAIN, at)
+                return carry[0] + fold(scaled), carry[1] + fold(scaled * normal)
+
+            one, two = over_rows(width, add_middle, (zero, zero))
+            back_out[chunk, pl.ds(2 * block, 1), :] = total(one)
+            back_out[chunk, pl.ds(2 * block + 1, 1), :] = total(two)
+
+        over_blocks(chunk, body)
+        begin("third", chunk)
+
+    def first_backward(chunk):
+        arrive("third", chunk)
+        back_in[chunk, me] = back_out[chunk]
+
+        def body(block, place):
+            mean_scaled = gathered(back_out, back_in, chunk, 2 * block) / D
+            mean_product = gathered(back_out, back_in, chunk, 2 * block + 1) / D
+            inverse = first_inverse[place]
+
+            def part(at, carry):
+                here = pl.ds(at, ROWS)
+                back = inverse * (
+                    second_sum[place, here, :] * column(FIRST_GAIN, at)
+                    - mean_scaled
+                    - first_sum[place, here, :] * mean_product
+                )
+                first_back_ref[place, here, :] = back
+                backs_out[place, here, :] = back.astype(BF16)
+                add_sum(BIAS_OUTPUT, at, back)
+                return carry
+
+            over_rows(width, part, 0)
+
+        over_blocks(chunk, body)
+        begin("backs", chunk)
+        backs_in[chunk, me] = backs_out[chunk * blocks + me]
+
+    def project_back(chunk):
+        arrive("backs", chunk)
+        back = dot(output_natural[...], backs_in[chunk].reshape(cols * width, BLOCK))
+        for group in range(cols):
+            context_back_out[chunk, group] = back[group * width : (group + 1) * width].astype(BF16)
+        begin("context_back", chunk)
+        context_back_ref[chunk * blocks + me] = context_back_out[chunk, me]
+        every = contexts[chunk].reshape(cols * width, BLOCK)
+        for part in range(rows):
+            fresh = dot_nt(every, backs_in[chunk, part])
+            if chunk == 0:
+                grad_output_ref[part] = fresh
+            else:
+                grad_output_ref[part] += fresh
+
+    for copy in weights[0::3]:
+        copy.wait_recv()
+    for group in range(cols):
+        here = slice(group * width, (group + 1) * width)
+        output_natural[here, :] = jnp.concatenate([output_parts[part, group] for part in range(rows)], axis=1)
+    for part in range(rows):
+        here = slice(part * width, (part + 1) * width)
+        output_turned[here, :] = jnp.concatenate(
+            [output_parts[part, group].T for group in range(cols)], axis=1
+        )
+    project(0)
+    for copy in weights[1::3] + weights[2::3]:
+        copy.wait_recv()
+    expand_natural[...] = jnp.concatenate([expand_parts[part] for part in range(rows)], axis=1)
+    for part in range(rows):
+        expand_turned[part * width : (part + 1) * width, :] = expand_parts[part].T
+    reduce_turned[...] = reduce_parts[...].reshape(reduce_turned.shape)
+    reduce_natural[...] = reduce_turned[...].T
+    project(1)
+    project(2)
+    add_first(0)
+    feed_forward(0)
+    add_first(1)
+    feed_back(0)
+    feed_forward(1)
+    first_backward(0)
+    add_first(2)
+    feed_back(1)
+    feed_forward(2)
+    first_backward(1)
+    project_back(0)
+    feed_back(2)
+    project_back(1)
+    first_backward(2)
+    project_back(2)
+    for chunk in range(chunks):
+        arrive("context_back", chunk)
+    for copy in weights:
+        copy.wait_send()
+    for kind in kinds:
+        for chunk in range(chunks):
+            for copy in transfers(kind, chunk):
+                copy.wait_send()
+
+
+def middle_part(rows, cols, turned, context, cotangent, output_weight, expand_weight, reduce_weight, vectors):
+    every, width, unused = turned.shape
+    blocks = LEN // BLOCK
+    chunks = every // blocks
+    wide = expand_weight.shape[1] * rows
+    most = max(rows, cols) - 1
+
+    def low(*shape):
+        return pltpu.VMEM(shape, BF16)
+
+    def full(*shape):
+        return pltpu.VMEM(shape, F32)
+
+    return pl.pallas_call(
+        functools.partial(middle_kernel, rows, cols),
+        out_shape=(
+            jax.ShapeDtypeStruct(cotangent.shape, BF16),
+            jax.ShapeDtypeStruct((every, width, BLOCK), F32),
+            jax.ShapeDtypeStruct((every, width, BLOCK), BF16),
+            jax.ShapeDtypeStruct((rows, cols * width, width), F32),
+            jax.ShapeDtypeStruct((wide, width), F32),
+            jax.ShapeDtypeStruct((width, wide), F32),
+            jax.ShapeDtypeStruct((6 + wide // width, width, 128), F32),
+        ),
+        in_specs=[vmem_spec()] * 7,
+        out_specs=(vmem_spec(),) * 7,
+        scratch_shapes=[
+            low(chunks, cols, width, BLOCK), low(chunks, cols, width, BLOCK), low(chunks, cols, width, BLOCK),
+            low(every, width, BLOCK), low(chunks, cols, width, BLOCK), low(chunks, cols, width, BLOCK),
+            full(chunks, 2 * blocks, BLOCK), full(chunks, cols, 2 * blocks, BLOCK),
+            full(chunks, 4 * blocks, BLOCK), full(chunks, cols, 4 * blocks, BLOCK),
+            full(chunks, 2 * blocks, BLOCK), full(chunks, cols, 2 * blocks, BLOCK),
+            low(rows, cols, width, width), low(rows, width, width), low(rows, *reduce_weight.shape),
+            low(D, D), low(D, D), low(width, wide), low(wide, width), low(wide, width), low(width, wide),
+            full(EXPAND_BIAS + wide // width, width, 128),
+            full(every, width, BLOCK), full(every, width, BLOCK), low(every, width, BLOCK), full(every, 1, BLOCK),
+            full(wide, BLOCK), low(every, wide, BLOCK), full(every, wide, BLOCK),
+            low(wide, BLOCK), full(width, BLOCK), low(width, BLOCK), low(every, width, BLOCK),
+            pltpu.SemaphoreType.DMA((3, most)), pltpu.SemaphoreType.DMA((3, most)),
+            pltpu.SemaphoreType.DMA((7, chunks, most)), pltpu.SemaphoreType.DMA((7, chunks, most)),
+        ],
+        compiler_params=pltpu.CompilerParams(
+            collective_id=1, has_side_effects=True, vmem_limit_bytes=VMEM_BYTES
+        ),
+        name="middle_part",
+    )(turned, context, cotangent, output_weight, expand_weight, reduce_weight, vectors)
+
+
+def reduce_kernel(
+    devices, rows, cols,
+    joined_ref, output_ref, expand_ref, reduce_ref, sums_ref, more_sums_ref,
+    query_out_ref, key_out_ref, value_out_ref, output_out_ref, expand_out_ref, reduce_out_ref, vectors_out_ref,
+    one_joined, one_output, one_expand, one_reduce, vectors_a,
+    got_joined, got_output, got_expand, got_reduce, got_vectors_a,
+    two_joined, two_output, two_expand, two_reduce, vectors_b,
+    far_joined, far_output, far_expand, far_reduce, got_vectors_b,
+    near_joined, near_output, near_expand, near_reduce,
+    col_output, col_got, last_output, last_joined, last_expand, last_reduce, vectors_c,
+    all_output, all_joined, all_expand, all_reduce, got_vectors_c,
+    send, recv, col_send, col_recv, last_send, last_recv,
+):
+    row, col, data = lax.axis_index("row"), lax.axis_index("col"), lax.axis_index("dp")
+    core, high = lax.rem(row, 2), row // 2
+    sibling, across = row + 1 - 2 * core, lax.rem(row + 2, rows)
+    width = expand_ref.shape[1]
+    part = width // rows
+    greet((("row", rows), ("col", cols), ("dp", devices)))
+
+    def joined_piece(kind, owner):
+        return joined_ref[kind, pl.ds(pl.multiple_of(owner * part, 8), part), :]
+
+    def expand_piece(owner):
+        return expand_ref[pl.ds(pl.multiple_of(owner * width, 8), width), :]
+
+    def reduce_piece(owner):
+        return reduce_ref[pl.ds(pl.multiple_of(owner * part, 8), part), :]
+
+    for side in range(2):
+        owner = 2 * side + 1 - core
+        for kind in range(3):
+            one_joined[side, kind] = joined_piece(kind, owner).astype(BF16)
+        one_output[side] = output_ref[owner].astype(BF16)
+        one_expand[side] = expand_piece(owner).astype(BF16)
+        one_reduce[side] = reduce_piece(owner).astype(BF16)
+    vectors_a[...] = jnp.zeros_like(vectors_a)
+    gathered = [sums_ref[kind] for kind in range(sums_ref.shape[0])]
+    gathered += [more_sums_ref[kind] for kind in range(more_sums_ref.shape[0])]
+    for kind, value in enumerate(gathered):
+        vectors_a[kind : kind + 1, :] = jnp.sum(value.T, axis=0, keepdims=True)
+    first = [
+        remote(source, target, send.at[0, index], recv.at[0, index], "row", sibling)
+        for index, (source, target) in enumerate(
+            ((one_output, got_output), (one_joined, got_joined), (one_expand, got_expand),
+             (one_reduce, got_reduce), (vectors_a, got_vectors_a))
+        )
+    ]
+    for copy in first:
+        copy.start()
+    for copy in first:
+        copy.wait_recv()
+    there, here = 1 - high, high
+    far, near = 2 * there + core, 2 * here + core
+    two_output[...] = (output_ref[far] + got_output[there].astype(F32)).astype(BF16)
+    for kind in range(3):
+        two_joined[kind] = (joined_piece(kind, far) + got_joined[there, kind].astype(F32)).astype(BF16)
+    two_expand[...] = (expand_piece(far) + got_expand[there].astype(F32)).astype(BF16)
+    two_reduce[...] = (reduce_piece(far) + got_reduce[there].astype(F32)).astype(BF16)
+    vectors_b[...] = vectors_a[...] + got_vectors_a[...]
+    second = [
+        remote(source, target, send.at[1, index], recv.at[1, index], "row", across)
+        for index, (source, target) in enumerate(
+            ((two_output, far_output), (two_joined, far_joined), (two_expand, far_expand),
+             (two_reduce, far_reduce), (vectors_b, got_vectors_b))
+        )
+    ]
+    for copy in second:
+        copy.start()
+    near_output[...] = output_ref[near] + got_output[here].astype(F32)
+    for kind in range(3):
+        near_joined[kind] = joined_piece(kind, near) + got_joined[here, kind].astype(F32)
+    near_expand[...] = expand_piece(near) + got_expand[here].astype(F32)
+    near_reduce[...] = reduce_piece(near) + got_reduce[here].astype(F32)
+
+    second[0].wait_recv()
+    summed = near_output[...] + far_output[...].astype(F32)
+    near_output[...] = summed
+    for group in range(cols):
+        col_output[group] = summed[group * width : (group + 1) * width].astype(BF16)
+    across_cols = []
+    for distance in range(1, cols):
+        peer = peer_of("col", cols, distance)
+        across_cols.append(
+            remote(col_output.at[peer], col_got.at[col], col_send.at[distance - 1], col_recv.at[distance - 1], "col", peer)
+        )
+    for copy in across_cols:
+        copy.start()
+
+    for copy in second[1:]:
+        copy.wait_recv()
+    for kind in range(3):
+        value = near_joined[kind] + far_joined[kind].astype(F32)
+        near_joined[kind] = value
+        last_joined[kind] = value.astype(BF16)
+    value = near_expand[...] + far_expand[...].astype(F32)
+    near_expand[...] = value
+    last_expand[...] = value.astype(BF16)
+    value = near_reduce[...] + far_reduce[...].astype(F32)
+    near_reduce[...] = value
+    last_reduce[...] = value.astype(BF16)
+    vectors_c[...] = vectors_b[...] + got_vectors_b[...]
+    last = []
+
+    def exchange(index, source, target):
+        for distance in range(1, devices):
+            peer = peer_of("dp", devices, distance)
+            copy = remote(
+                source, target.at[data], last_send.at[index, distance - 1], last_recv.at[index, distance - 1], "dp", peer
+            )
+            copy.start()
+            last.append(copy)
+
+    exchange(1, last_joined, all_joined)
+    exchange(2, last_expand, all_expand)
+    exchange(3, last_reduce, all_reduce)
+    exchange(4, vectors_c, got_vectors_c)
+
+    for copy in across_cols:
+        copy.wait_recv()
+    own = near_output[pl.ds(pl.multiple_of(col * width, 8), width), :]
+    for distance in range(1, cols):
+        own += col_got[source_of("col", cols, distance)].astype(F32)
+    last_output[...] = own.astype(BF16)
+    exchange(0, last_output, all_output)
+    for copy in last:
+        copy.wait_recv()
+    joined = [near_joined[kind] for kind in range(3)]
+    expand, reduce, vectors = near_expand[...], near_reduce[...], vectors_c[...]
+    for distance in range(1, devices):
+        source = source_of("dp", devices, distance)
+        own += all_output[source].astype(F32)
+        joined = [joined[kind] + all_joined[source, kind].astype(F32) for kind in range(3)]
+        expand += all_expand[source].astype(F32)
+        reduce += all_reduce[source].astype(F32)
+        vectors += got_vectors_c[source]
+    query_out_ref[...] = joined[0]
+    key_out_ref[...] = joined[1]
+    value_out_ref[...] = joined[2]
+    output_out_ref[...] = own
+    expand_out_ref[...] = expand.T
+    reduce_out_ref[...] = reduce
+    vectors_out_ref[...] = vectors
+    for copy in first + second + across_cols + last:
+        copy.wait_send()
+
+
+def reduce_gradients(devices, rows, cols, joined, output, expand, reduce, sums, more_sums):
+    width = joined.shape[1]
+    part = width // rows
+    wide = expand.shape[0]
+    count = 16
+
+    def low(*shape):
+        return pltpu.VMEM(shape, BF16)
+
+    def full(*shape):
+        return pltpu.VMEM(shape, F32)
+
+    piece = (3, part, width)
+    shapes = (piece, (cols * width, width), (width, width), (part, wide))
+    vectors = (count, width)
+    return pl.pallas_call(
+        functools.partial(reduce_kernel, devices, rows, cols),
+        out_shape=tuple(
+            jax.ShapeDtypeStruct(shape, F32)
+            for shape in ((part, width),) * 3 + ((width, width), (width, width), (part, wide), vectors)
+        ),
+        in_specs=[vmem_spec()] * 6,
+        out_specs=(vmem_spec(),) * 7,
+        scratch_shapes=[
+            *(low(2, *shape) for shape in shapes), full(*vectors),
+            *(low(2, *shape) for shape in shapes), full(*vectors),
+            *(low(*shape) for shape in shapes), full(*vectors),
+            *(low(*shape) for shape in shapes), full(*vectors),
+            *(full(*shape) for shape in shapes),
+            low(cols, width, width), low(cols, width, width),
+            low(width, width), low(*piece), low(width, width), low(part, wide), full(*vectors),
+            low(devices, width, width), low(devices, *piece), low(devices, width, width),
+            low(devices, part, wide), full(devices, *vectors),
+            pltpu.SemaphoreType.DMA((2, 5)), pltpu.SemaphoreType.DMA((2, 5)),
+            pltpu.SemaphoreType.DMA((cols - 1,)), pltpu.SemaphoreType.DMA((cols - 1,)),
+            pltpu.SemaphoreType.DMA((5, devices - 1)), pltpu.SemaphoreType.DMA((5, devices - 1)),
+        ],
+        compiler_params=pltpu.CompilerParams(
+            collective_id=2, has_side_effects=True, vmem_limit_bytes=VMEM_BYTES
+        ),
+        name="reduce_gradients",
+    )(joined, output, expand, reduce, sums, more_sums)
 
 
 def local(
-    inputs,
-    segment_ids,
-    keep_mask,
-    query_weight,
-    query_bias,
-    key_weight,
-    value_weight,
-    value_bias,
-    output_weight,
-    output_bias,
-    first_gain,
-    first_shift,
-    expand_weight,
-    expand_bias,
-    reduce_weight,
-    reduce_bias,
-    second_gain,
-    second_shift,
-    cotangent,
+    devices, rows, cols,
+    inputs, segment_ids, keep_mask, query_weight, query_bias, key_weight, value_weight, value_bias,
+    output_weight, output_bias, first_gain, first_shift, expand_weight, expand_bias, reduce_weight,
+    reduce_bias, second_gain, second_shift, cotangent,
 ):
-    pairs = inputs[:, 0, :]
-    inputs = as_rows(inputs)
-    cotangent = as_rows(cotangent)
-    query_full, key_full, value_full, output_full, expand_full, reduce_full = (
-        lax.all_gather(query_weight, "row", axis=1, tiled=True),
-        lax.all_gather(key_weight, "row", axis=1, tiled=True),
-        lax.all_gather(value_weight, "row", axis=1, tiled=True),
-        lax.all_gather(output_weight, "row", axis=1, tiled=True),
-        lax.all_gather(expand_weight, "row", axis=1, tiled=True),
-        lax.all_gather(reduce_weight, "row", axis=1, tiled=True),
-    )
+    pairs, cotangent_pairs = inputs[:, 0, :], cotangent[:, 0, :]
+    width = query_bias.shape[0]
     every = segment_ids.shape[0] // BLOCK
     coded = jnp.stack([segment_ids, jnp.where(keep_mask == 1, segment_ids, -1)]).astype(F32)
     coded = coded.reshape(2, every, PAIRS, 2).transpose(1, 0, 3, 2).reshape(every, 2, BLOCK)
     codes = jnp.pad(coded, ((0, 0), (0, 6), (0, 0)))
-    weight = jnp.stack([query_full.T, key_full.T, value_full.T])
-    vectors = jnp.pad(jnp.stack([query_bias, value_bias]), ((0, 6), (0, 0)))
-    turned, joined, context_t, logsums = attention_forward(pairs, segment_ids, keep_mask, weight, vectors, codes)
-    context = rows_of(context_t)
-    attended = lax.psum_scatter(
-        forward_product(context, output_full).astype(jnp.bfloat16),
-        "col",
-        scatter_dimension=1,
-        tiled=True,
-    ).astype(jnp.float32)
-    middle, first_normal, first_inverse = norm_forward(
-        inputs.astype(jnp.float32) + attended + output_bias, first_gain, first_shift
+    stacked = [
+        query_bias, value_bias, output_bias, first_gain, first_shift, reduce_bias, second_gain, second_shift,
+    ]
+    vectors = jnp.concatenate([jnp.stack(stacked), expand_bias.reshape(-1, width)])
+    vectors = jnp.pad(vectors, ((0, -vectors.shape[0] % 8), (0, 0)))
+    weight, output_blocks = gather_weights(
+        rows, cols, query_weight.T, key_weight.T, value_weight.T, output_weight
     )
-    middle_low = middle.astype(jnp.bfloat16)
-    expanded = forward_product(middle_low, expand_full) + expand_bias
-    activated = jax.nn.gelu(expanded, approximate=False).astype(jnp.bfloat16)
-    reduced = forward_product(activated, reduce_full)
-    result, second_normal, second_inverse = norm_forward(
-        middle + reduced + reduce_bias, second_gain, second_shift
+    weight = weight.reshape(3, width, width)
+    turned, joined, context, logsums = attention_forward(pairs, segment_ids, keep_mask, weight, vectors, codes)
+    result, first_back, context_back, grad_output, grad_expand, grad_reduce, sums = middle_part(
+        rows, cols, turned, context, cotangent_pairs, output_blocks, expand_weight, reduce_weight.T, vectors
     )
-    second_back, gain_second, shift_second = norm_backward(
-        cotangent.astype(jnp.float32), second_normal, second_inverse, second_gain
+    input_grad, grad_joined, more_sums = attention_backward(
+        segment_ids, keep_mask, turned, joined, context, logsums, context_back, first_back, weight, codes
     )
-    bias_reduce = jnp.sum(second_back, axis=0)
-    reduced_back = second_back.astype(jnp.bfloat16)
-    activated_back = product_transposed(reduced_back, reduce_full)
-    grad_reduce = product_over_rows(activated, reduced_back)
-    gelu_slope = 0.5 * (1.0 + lax.erf(expanded * ROOT_HALF)) + expanded * DENSITY_SCALE * jnp.exp(
-        -0.5 * expanded * expanded
+    query, key, value, output, expand, reduce, found = reduce_gradients(
+        devices, rows, cols, grad_joined, grad_output, grad_expand, grad_reduce, sums, more_sums
     )
-    expanded_back = (activated_back * gelu_slope).astype(jnp.bfloat16)
-    bias_expand = jnp.sum(expanded_back.astype(jnp.float32), axis=0)
-    grad_expand = product_over_rows(middle_low, expanded_back)
-    middle_back = second_back + product_transposed(expanded_back, expand_full)
-    first_back, gain_first, shift_first = norm_backward(
-        middle_back, first_normal, first_inverse, first_gain
+    count = sums.shape[0]
+    return (
+        result[:, None, :], input_grad[:, None, :],
+        query.T, found[count], key.T, value.T, found[count + 1], output, found[BIAS_OUTPUT],
+        found[GAIN_FIRST], found[SHIFT_FIRST], expand, found[BIAS_EXPAND:count].reshape(-1), reduce.T,
+        found[BIAS_REDUCE], found[GAIN_SECOND], found[SHIFT_SECOND],
     )
-    bias_output = jnp.sum(first_back, axis=0)
-    attended_back = first_back.astype(jnp.bfloat16)
-    upstream_whole = lax.all_gather(attended_back, "col", axis=1, tiled=True)
-    context_grad = product_transposed(upstream_whole, output_full)
-    grad_output = product_over_rows(context, upstream_whole)
-    input_grad, weight_grad, bias_grad = attention_backward(
-        segment_ids, keep_mask, turned, joined, context_t, logsums, columns_from(context_grad.astype(BF16)),
-        columns_from(first_back), weight, codes)
-    bias_query = jnp.sum(bias_grad[0], axis=1)
-    bias_value = jnp.sum(bias_grad[1], axis=1)
-    grad_query, grad_key, grad_value = weight_grad[0].T, weight_grad[1].T, weight_grad[2].T
-    row_devices = lax.axis_size("row")
-    scattered = (
-        lax.psum_scatter(
-            grad_query.astype(jnp.bfloat16), "row", scatter_dimension=1, tiled=True
-        ).astype(jnp.float32),
-        lax.psum_scatter(
-            grad_key.astype(jnp.bfloat16), "row", scatter_dimension=1, tiled=True
-        ).astype(jnp.float32),
-        lax.psum_scatter(
-            grad_value.astype(jnp.bfloat16), "row", scatter_dimension=1, tiled=True
-        ).astype(jnp.float32),
-        lax.psum_scatter(
-            grad_output.astype(jnp.bfloat16), "row", scatter_dimension=1, tiled=True
-        ).astype(jnp.float32),
-        lax.psum_scatter(
-            grad_expand.astype(jnp.bfloat16), "row", scatter_dimension=1, tiled=True
-        ).astype(jnp.float32),
-        lax.psum_scatter(
-            grad_reduce.astype(jnp.bfloat16), "row", scatter_dimension=1, tiled=True
-        ).astype(jnp.float32),
-        lax.psum_scatter(
-            spread(bias_query, row_devices).astype(jnp.bfloat16),
-            "row",
-            scatter_dimension=1,
-            tiled=True,
-        ).astype(jnp.float32),
-        lax.psum_scatter(
-            spread(bias_value, row_devices).astype(jnp.bfloat16),
-            "row",
-            scatter_dimension=1,
-            tiled=True,
-        ).astype(jnp.float32),
-        lax.psum_scatter(
-            spread(bias_output, row_devices).astype(jnp.bfloat16),
-            "row",
-            scatter_dimension=1,
-            tiled=True,
-        ).astype(jnp.float32),
-        lax.psum_scatter(
-            spread(gain_first, row_devices).astype(jnp.bfloat16),
-            "row",
-            scatter_dimension=1,
-            tiled=True,
-        ).astype(jnp.float32),
-        lax.psum_scatter(
-            spread(shift_first, row_devices).astype(jnp.bfloat16),
-            "row",
-            scatter_dimension=1,
-            tiled=True,
-        ).astype(jnp.float32),
-        lax.psum_scatter(
-            spread(bias_expand, row_devices).astype(jnp.bfloat16),
-            "row",
-            scatter_dimension=1,
-            tiled=True,
-        ).astype(jnp.float32),
-        lax.psum_scatter(
-            spread(bias_reduce, row_devices).astype(jnp.bfloat16),
-            "row",
-            scatter_dimension=1,
-            tiled=True,
-        ).astype(jnp.float32),
-        lax.psum_scatter(
-            spread(gain_second, row_devices).astype(jnp.bfloat16),
-            "row",
-            scatter_dimension=1,
-            tiled=True,
-        ).astype(jnp.float32),
-        lax.psum_scatter(
-            spread(shift_second, row_devices).astype(jnp.bfloat16),
-            "row",
-            scatter_dimension=1,
-            tiled=True,
-        ).astype(jnp.float32),
-    )
-    summed = (
-        lax.psum(scattered[0].astype(jnp.bfloat16), "dp").astype(jnp.float32),
-        lax.psum(scattered[1].astype(jnp.bfloat16), "dp").astype(jnp.float32),
-        lax.psum(scattered[2].astype(jnp.bfloat16), "dp").astype(jnp.float32),
-        lax.psum(scattered[3].astype(jnp.bfloat16), "dp").astype(jnp.float32),
-        lax.psum(scattered[4].astype(jnp.bfloat16), "dp").astype(jnp.float32),
-        lax.psum(scattered[5].astype(jnp.bfloat16), "dp").astype(jnp.float32),
-        lax.psum(scattered[6][:, 0].astype(jnp.bfloat16), "dp").astype(jnp.float32),
-        lax.psum(scattered[7][:, 0].astype(jnp.bfloat16), "dp").astype(jnp.float32),
-        lax.psum(scattered[8][:, 0].astype(jnp.bfloat16), "dp").astype(jnp.float32),
-        lax.psum(scattered[9][:, 0].astype(jnp.bfloat16), "dp").astype(jnp.float32),
-        lax.psum(scattered[10][:, 0].astype(jnp.bfloat16), "dp").astype(jnp.float32),
-        lax.psum(scattered[11][:, 0].astype(jnp.bfloat16), "dp").astype(jnp.float32),
-        lax.psum(scattered[12][:, 0].astype(jnp.bfloat16), "dp").astype(jnp.float32),
-        lax.psum(scattered[13][:, 0].astype(jnp.bfloat16), "dp").astype(jnp.float32),
-        lax.psum(scattered[14][:, 0].astype(jnp.bfloat16), "dp").astype(jnp.float32),
-    )
-    return (
-        as_pairs(result.astype(jnp.bfloat16)),
-        input_grad[:, None, :],
-        summed[0],
-        summed[6],
-        summed[1],
-        summed[2],
-        summed[7],
-        summed[3],
-        summed[8],
-        summed[9],
-        summed[10],
-        summed[4],
-        summed[11],
-        summed[5],
-        summed[12],
-        summed[13],
-        summed[14],
-    )
 
 
 def solution(mesh):
-    placed = (
-        P(("dp", "row"), "col", None),
-        P(("dp", "row")),
-        P(("dp", "row")),
-        P("col", "row"),
-        P("col"),
-        P("col", "row"),
-        P("col", "row"),
-        P("col"),
-        P("col", "row"),
-        P("col"),
-        P("col"),
-        P("col"),
-        P("col", "row"),
-        P("col"),
-        P("col", "row"),
-        P("col"),
-        P("col"),
-        P("col"),
-        P(("dp", "row"), "col", None),
-    )
+    tokens, weight, vector = P(("dp", "row"), "col", None), P("col", "row"), P("col")
+    ids = P(("dp", "row"))
     return jax.shard_map(
-        local,
+        functools.partial(local, mesh.shape["dp"], mesh.shape["row"], mesh.shape["col"]),
         mesh=mesh,
-        in_specs=placed,
+        in_specs=(
+            tokens, ids, ids, weight, vector, weight, weight, vector, weight, vector, vector, vector, weight,
+            vector, weight, vector, vector, vector, tokens,
+        ),
         out_specs=(
-            P(("dp", "row"), "col", None),
-            P(("dp", "row"), "col", None),
-            P("col", "row"),
-            P("col"),
-            P("col", "row"),
-            P("col", "row"),
-            P("col"),
-            P("col", "row"),
-            P("col"),
-            P("col"),
-            P("col"),
-            P("col", "row"),
-            P("col"),
-            P("col", "row"),
-            P("col"),
-            P("col"),
-            P("col"),
+            tokens, tokens, weight, vector, weight, weight, vector, weight, vector, vector, vector, weight,
+            vector, weight, vector, vector, vector,
         ),
         check_vma=False,
     )

time: 551 us -> 285 us (0.52)
  Pallas kernels: 68.2 us -> 261 us
  waiting for transfers between devices: 171 us -> 0 us
  blocking collectives: 126 us -> 0 us
  matrix products: 62.9 us -> 0 us
  local copies, waits for them, and re-layouts: 66.2 us -> 17.7 us
  other arithmetic: 31.9 us -> 0.74 us
  between operations: 15 us -> 0.79 us
    pallas_call x0 -> x3, Pallas kernels: none -> 202 us  [the longest x1 153 us: middle_part(): pl.pallas_call(functools.partial(middle_kernel, rows, cols), out_shape=(j...]
    reduce_scatter x5 -> x0, waiting for transfers between devices: 92.1 us -> none  [the longest x1 62 us: local(): lax.psum_scatter(forward_product(context, output_full).astype(jnp.bfloat1...]
    psum x5 -> x0, blocking collectives: 78.6 us -> none  [the longest x2 34.7 us: norm_forward(): lax.psum((jnp.sum(summed, axis=1), jnp.sum(summed * summed, axis=1)), 'col')]
    all_gather x1 -> x0, waiting for transfers between devices: 68.4 us -> none  [local(): upstream_whole = lax.all_gather(attended_back, 'col', axis=1, tiled=True)]
    dot_general x9 -> x0, matrix products: 62.9 us -> none  [the longest x3 31 us: forward_product(): return jnp.dot(left, right, preferred_element_type=jnp.float32)]
    all_gather x6 -> x0, blocking collectives: 37.4 us -> none  [the longest x1 7.28 us: local(): lax.all_gather(reduce_weight, 'row', axis=1, tiled=True)]
    reshape x10 -> x2, local copies, waits for them, and re-layouts: 24.4 us -> 1.44 us  [the longest x1 0.77 us: local(): expand_bias.reshape(-1, width)]
    reduce_sum x6 -> x0, other arithmetic: 15.5 us -> none  [the longest x2 4.77 us: norm_backward(): return (back, jnp.sum(upstream * normal, axis=0), jnp.sum(upstream, axis=0))]
  transfers between devices with their start and end apart: 9 -> 0, of which waited for: 5 -> 0; matrix products, arithmetic and copies ran while one was open for 16% -> 0% of each run, Pallas kernels for 8% -> 0%
where the time goes in v2:
time: 285 us; the launch traced here: 280 us
  Pallas kernels  261 us (92%)
  local copies, waits for them, and re-layouts  17.7 us (6%)
    pallas_call x1, Pallas kernels, middle_part(): pl.pallas_call(functools.partial(middle_kernel, rows, cols), out_shape=(j...  153 us
    pallas_call x1, Pallas kernels, attention_backward(): pl.pallas_call(backward_kernel, out_shape=(jax.ShapeDtypeStruct((sequence...  36.6 us
    pallas_call x1, Pallas kernels, reduce_gradients(): pl.pallas_call(functools.partial(reduce_kernel, devices, rows, cols), out...  33.7 us
    pallas_call x1, Pallas kernels, attention_forward(): pl.pallas_call(forward_kernel, out_shape=(jax.ShapeDtypeStruct((every, wi...  22.6 us
    pallas_call x1, Pallas kernels, gather_weights(): pl.pallas_call(functools.partial(gather_kernel, rows, cols), out_shape=(j...  15.6 us
    unnamed x26, local copies, waits for them, and re-layouts  11.5 us

profile of v2, /device:TPU:0, one launch (start us, length us, event | category | flops | bytes accessed | tf_op | source)
XLA Modules:
  0.0 280.3 jit_solution(18217702809932592596)
XLA Ops:
  0.7 0.0 copy-start.1
  0.7 0.8 reshape.52
  1.4 0.8 concatenate.4
  2.3 0.6 pad.8.vectors_ref
  2.9 0.7 compare_select_fusion
  3.6 15.6 %gather_weights.1 = (bf16[3,4,48,192]{3,2,1,0:T(8,128)(2,1)}, bf16[4,192,192]{2,1,0:T(8,128)(2,1)}) custom-call(bf16[48,192]{1,0:T(8,128)(2,1)} %bitcast.42, bf16[48,192]{1,0:T(8,128)(2,1)} %bitcast.43, bf16[48,192]{1,0:T(8,128)(2,1)} %bitcast.44, bf16[192,192]{1,0:T(8,128)(2,1)} %output_ref.1), custom_call_target="tpu_custom_call" | custom-call | tf_op jit(solution)/shard_map/gather_weights/pallas_call | solution.py:383
  19.2 0.7 stack.42
  19.9 0.3 copy.40
  20.2 0.0 copy-done.1
  20.2 0.7 stack.41
  20.9 0.3 copy.39
  21.3 0.7 pad.9.codes_ref
  21.9 22.6 %attention_forward.1 = (bf16[12,192,256]{2,1,0:T(8,128)(2,1)}, bf16[12,3,192,256]{3,2,1,0:T(8,128)(2,1)}, bf16[12,192,256]{2,1,0:T(8,128)(2,1)}, f32[12,8,256]{2,1,0:T(8,128)}) custom-call(s32[3072]{0:T(1024)} %segment_ref.3, s32[3072]{0:T(1024)} %keep_ref.3, bf16[1536,384]{1,0:T(8,128)(2,1)} %bitcast.34, bf16[3,192,192]{2,1,0:T(8,128)(2,1)} %bitcast.32, ...), custom_call_target="tpu_custom_call" | custom-call | tf_op jit(solution)/shard_map/attention_forward/pallas_call | solution.py:159
  44.6 152.7 %middle_part.1 = (bf16[1536,384]{1,0:T(8,128)(2,1)}, f32[12,192,256]{2,1,0:T(8,128)}, bf16[12,192,256]{2,1,0:T(8,128)(2,1)}, f32[4,768,192]{2,1,0:T(8,128)}, f32...) custom-call(bf16[12,192,256]{2,1,0:T(8,128)(2,1)} %get-tuple-element.41.turned_ref, ...), custom_call_target="tpu_custom_call" | custom-call | tf_op jit(solution)/shard_map/middle_part/pallas_call | solution.py:773
  197.3 36.6 %attention_backward.1 = (f32[1536,384]{1,0:T(8,128)}, f32[3,192,192]{2,1,0:T(8,128)}, f32[2,192,128]{2,1,0:T(8,128)}) custom-call(s32[3072]{0:T(1024)} %segment_ref.3, s32[3072]{0:T(1024)} %keep_ref.3, bf16[12,192,256]{2,1,0:T(8,128)(2,1)} %get-tuple-element.41.turned_ref, bf16[12,3,192,256]{3,2,1,0:T(8,128)(2,1)} %get-tuple-element.45.joined_ref, ...), custom_call_target="tpu_custom_call" | custom-call | tf_op jit(solution)/shard_map/attention_backward/pallas_call | solution.py:290
  233.8 33.7 %reduce_gradients.1 = (f32[48,192]{1,0:T(8,128)}, f32[48,192]{1,0:T(8,128)}, f32[48,192]{1,0:T(8,128)}, f32[192,192]{1,0:T(8,128)}, f32[192,192]{1,0:T(8,128)}, /*index=5*/f32[48,768]{1,0:T(8,128)}, f32[16,192]{1,0:T(8,128)}) custom-call(f32[3,192,192]{2,1,0:T(8,128)} %get-tuple-element.50.joined_ref, f32[4,768,192]{2,1,0:T(8,128)} %get-tuple-element.51.output_ref, ...), custom_call_target="tpu_custom_call" | custom-call | tf_op jit(solution)/shard_map/reduce_gradients/pallas_call | solution.py:970
  267.5 0.0 copy-start.8
  267.5 0.0 copy-start
  267.5 6.6 %copy.42 = f32[1536,1,384]{2,1,0:T(1,128)} copy(f32[1536,1,384]{2,0,1:T(8,128)} %bitcast.31) | data formatting | bytes 4718592
  274.1 0.0 copy-done.8
  274.1 0.6 fusion.1
  274.7 0.7 reshape.54
  275.4 0.0 copy-done
  275.4 0.0 copy-start.3
  275.4 0.0 copy-start.2
  275.4 1.0 copy.50
  276.4 0.6 copy.51
  277.1 0.6 copy.52
  277.7 0.6 copy.53
  278.3 0.7 copy.54
  279.0 0.7 copy.55
  279.7 0.7 copy.56
  (14 shorter events, 0.1 us)
Async XLA Ops:
  0.7 19.5 %copy-start.1 = (s32[3072]{0:T(1024)S(1)}, s32[3072]{0:T(1024)}, u32[]{:S(2)}) copy-start(s32[3072]{0:T(1024)} %segment_ref.3) | copy-start | bytes 36868
  267.5 6.6 %copy-start.8 = (f32[16,192]{1,0:T(8,128)S(1)}, f32[16,192]{1,0:T(8,128)}, u32[]{:S(2)}) copy-start(f32[16,192]{1,0:T(8,128)} %get-tuple-element.57) | copy-start | bytes 36868
  267.5 7.9 %copy-start = (bf16[1536,384]{1,0:T(8,128)(2,1)S(1)}, bf16[1536,384]{1,0:T(8,128)(2,1)}, u32[]{:S(2)}) copy-start(bf16[1536,384]{1,0:T(8,128)(2,1)} %get-tuple-element.44) | copy-start | bytes 3538948
  275.4 1.1 copy-start.7
  275.4 1.7 copy-start.6
  275.4 2.3 copy-start.5
  275.4 2.9 %copy-start.3 = (f32[192,192]{1,0:T(8,128)S(1)}, f32[192,192]{1,0:T(8,128)}, u32[]{:S(2)}) copy-start(f32[192,192]{1,0:T(8,128)} %get-tuple-element.146) | copy-start | bytes 442372
  275.4 3.6 %copy-start.2 = (f32[192,192]{1,0:T(8,128)S(1)}, f32[192,192]{1,0:T(8,128)}, u32[]{:S(2)}) copy-start(f32[192,192]{1,0:T(8,128)} %get-tuple-element.150) | copy-start | bytes 442372
  275.4 4.3 %copy-start.4 = (f32[48,768]{1,0:T(8,128)S(1)}, f32[48,768]{1,0:T(8,128)}, u32[]{:S(2)}) copy-start(f32[48,768]{1,0:T(8,128)} %get-tuple-element.62) | copy-start | bytes 442372

commit v3 on v2

v3 whole, which is shorter than its diff:
```python
import functools

import jax
import jax.numpy as jnp
from jax import lax
from jax.experimental import pallas as pl
from jax.experimental.pallas import tpu as pltpu
from jax.sharding import PartitionSpec as P

MESH = pl.DeviceIdType.MESH
BF16 = jnp.bfloat16
F32 = jnp.float32

D = 768
HEAD_DIM = 64
LEN = 1024
BLOCK = 256
PAIRS = BLOCK // 2
EPSILON = 1e-05
NEGATIVE = -1e30
ROOT_HALF = 0.7071067811865476
DENSITY_SCALE = 0.3989422804014327
VMEM_BYTES = 62 * 1024 * 1024


def dot(left, right):
    return jnp.dot(left, right, preferred_element_type=F32)


def dot_nt(left, right):
    return lax.dot_general(left, right, (((1,), (1,)), ((), ())), preferred_element_type=F32)


def columns_of(pairs):
    width = pairs.shape[1] // 2
    turned = pairs.T
    return jnp.concatenate([turned[:width], turned[width:]], axis=1)


def pairs_of(columns):
    half = columns.shape[1] // 2
    return jnp.concatenate([columns[:, :half], columns[:, half:]], axis=0).T


def vmem_spec():
    return pl.BlockSpec(memory_space=pltpu.VMEM)


def block_bias(key_codes, codes_ref, query_place, key_block, shift):
    keys = key_codes[key_block]
    keys = jnp.concatenate([keys, keys], axis=1)
    queries = codes_ref[query_place, 0:1, :]
    place = lax.broadcasted_iota(jnp.int32, (BLOCK, BLOCK), 0) - lax.broadcasted_iota(
        jnp.int32, (BLOCK, BLOCK), 1
    )
    return jnp.where((keys == queries) | (place == shift * BLOCK), 0.0, NEGATIVE)


def peer_of(axis, size, distance):
    return lax.rem(lax.axis_index(axis) + distance, size)


def source_of(axis, size, distance):
    return lax.rem(lax.axis_index(axis) + size - distance, size)


def greet(axes):
    barrier = pltpu.get_barrier_semaphore()
    count = 0
    for axis, size in axes:
        for distance in range(1, size):
            pl.semaphore_signal(
                barrier, inc=1, device_id={axis: peer_of(axis, size, distance)}, device_id_type=MESH
            )
            count += 1
    pl.semaphore_wait(barrier, count)


def remote(source, target, send_sem, recv_sem, axis, peer):
    return pltpu.make_async_remote_copy(
        src_ref=source, dst_ref=target, send_sem=send_sem, recv_sem=recv_sem,
        device_id={axis: peer}, device_id_type=MESH,
    )


ROWS = 32
QUERY_BIAS, VALUE_BIAS, OUTPUT_BIAS, FIRST_GAIN, FIRST_SHIFT, REDUCE_BIAS, SECOND_GAIN, SECOND_SHIFT, EXPAND_BIAS = range(9)
GAIN_SECOND, SHIFT_SECOND, BIAS_REDUCE, GAIN_FIRST, SHIFT_FIRST, BIAS_OUTPUT, BIAS_EXPAND = range(7)


def fold(value):
    return jnp.sum(value.reshape(value.shape[0] // 8, 8, value.shape[1]), axis=0)


def halves(value):
    return value[:, :128] + value[:, 128:]


def layer_kernel(
    devices, rows, cols,
    pairs_ref, cotangent_ref, codes_ref, vectors_ref, query_weight_ref, key_weight_ref, value_weight_ref,
    output_weight_ref, expand_weight_ref, reduce_weight_ref,
    result_ref, input_grad_ref, query_out_ref, key_out_ref, value_out_ref, output_out_ref, expand_out_ref,
    reduce_out_ref, vectors_out_ref,
    turned, joined, context, logsums, key_codes, key_rows, value_rows, value_turned, scaled, totals, deltas,
    joined_weight, joined_turned, joined_grad, context_back,
    grad_output, grad_expand, grad_reduce, sums,
    contexts, spread_out, spread_in,
    stat_out, stat_in, wide_out, wide_in, back_out, back_in,
    output_columns, output_parts, expand_parts, reduce_parts,
    output_natural, output_turned, expand_natural, expand_turned, reduce_natural, reduce_turned,
    columns, first_sum, second_sum, middle_low, first_inverse, hidden, activated, slope,
    hidden_back, narrow, low_rows,
    one_joined, one_output, one_expand, one_reduce, vectors_a,
    got_joined, got_output, got_expand, got_reduce, got_vectors_a,
    two_joined, two_output, two_expand, two_reduce, vectors_b,
    far_joined, far_output, far_expand, far_reduce, got_vectors_b,
    near_joined, near_output, near_expand, near_reduce,
    col_output, col_got, col_full, last_output, last_joined, last_expand, last_reduce, vectors_c,
    all_output, all_joined, all_expand, all_reduce, got_vectors_c,
    weight_send, weight_recv, send, recv, grad_send, grad_recv, col_send, col_recv, last_send, last_recv,
):
    row, me, data = lax.axis_index("row"), lax.axis_index("col"), lax.axis_index("dp")
    width = turned.shape[1]
    heads = width // HEAD_DIM
    blocks = LEN // BLOCK
    chunks = turned.shape[0] // blocks
    scale = HEAD_DIM ** (-0.5)
    greet((("row", rows), ("col", cols), ("dp", devices)))

    joined_copies, output_copies, other_copies, row_copies = [], [], [], []
    for distance in range(1, rows):
        peer = peer_of("row", rows, distance)
        for kind, ref in enumerate((query_weight_ref, key_weight_ref, value_weight_ref)):
            place = (kind, distance - 1)
            joined_copies.append(
                remote(ref, joined_weight.at[kind, row], weight_send.at[place], weight_recv.at[place], "row", peer)
            )
        for kind, source, target in ((3, expand_weight_ref, expand_parts), (4, reduce_weight_ref, reduce_parts)):
            place = (kind, distance - 1)
            other_copies.append(
                remote(source, target.at[row], weight_send.at[place], weight_recv.at[place], "row", peer)
            )
        place = (5, distance - 1)
        row_copies.append(
            remote(output_columns, output_parts.at[row], weight_send.at[place], weight_recv.at[place], "row", peer)
        )
    for distance in range(1, cols):
        peer = peer_of("col", cols, distance)
        place = (6, distance - 1)
        output_copies.append(
            remote(output_weight_ref, output_columns.at[me], weight_send.at[place], weight_recv.at[place], "col", peer)
        )
    for copy in joined_copies + output_copies + other_copies:
        copy.start()
    for kind, ref in enumerate((query_weight_ref, key_weight_ref, value_weight_ref)):
        joined_weight[kind, row] = ref[...]
    output_columns[me] = output_weight_ref[...]
    expand_parts[row] = expand_weight_ref[...]
    reduce_parts[row] = reduce_weight_ref[...]

    turned_vectors = vectors_ref[...].T
    for kind in range(columns.shape[0]):
        columns[kind] = jnp.broadcast_to(turned_vectors[:, kind : kind + 1], (width, 128))
    sums[...] = jnp.zeros_like(sums)
    grad_expand[...] = jnp.zeros_like(grad_expand)
    grad_reduce[...] = jnp.zeros_like(grad_reduce)
    joined_grad[...] = jnp.zeros_like(joined_grad)

    def turn(block, carry):
        here = pl.ds(pl.multiple_of(block * PAIRS, PAIRS), PAIRS)
        turned[block] = columns_of(pairs_ref[here, :])
        result_ref[block] = columns_of(cotangent_ref[here, :])
        return carry

    lax.fori_loop(0, chunks * blocks, turn, 0)

    def wide_column(kind):
        part = columns[kind]
        return jnp.concatenate([part, part], axis=1)

    def turn_heads(kind, target, block, place):
        for head in range(heads):
            target[head, block] = joined[place, kind, head * HEAD_DIM : (head + 1) * HEAD_DIM, :].T

    kinds = ("contexts", "attended", "first", "second", "third", "backs", "context_back")

    def transfers(kind, chunk):
        made = []
        for distance in range(1, cols):
            peer = peer_of("col", cols, distance)
            place = (kinds.index(kind), chunk, distance - 1)
            if kind == "contexts":
                source, target = context.at[chunk * blocks + peer], contexts.at[chunk, me]
            elif kind == "attended":
                source, target = spread_out.at[chunk, peer], spread_in.at[chunk, me]
            elif kind == "first":
                source, target = stat_out.at[chunk], stat_in.at[chunk, me]
            elif kind == "second":
                source, target = wide_out.at[chunk], wide_in.at[chunk, me]
            elif kind == "third":
                source, target = back_out.at[chunk], back_in.at[chunk, me]
            elif kind == "backs":
                source, target = middle_low.at[chunk * blocks + peer], spread_in.at[chunk, me]
            else:
                source, target = spread_out.at[chunk, peer], context_back.at[chunk * blocks + me]
            made.append(remote(source, target, send.at[place], recv.at[place], "col", peer))
        return made

    def begin(kind, chunk):
        for copy in transfers(kind, chunk):
            copy.start()

    def arrive(kind, chunk):
        for copy in transfers(kind, chunk):
            copy.wait_recv()

    def column(kind, at):
        part = columns[kind, pl.ds(at, ROWS), :]
        return jnp.concatenate([part, part], axis=1)

    def over_rows(count, body, carry):
        def step(index, carry):
            return body(pl.multiple_of(index * ROWS, ROWS), carry)

        return lax.fori_loop(0, count // ROWS, step, carry)

    def total(value):
        return jnp.sum(value, axis=0, keepdims=True)

    def add_sum(kind, at, value):
        sums[kind, pl.ds(at, ROWS), :] += halves(value)

    def over_blocks(chunk, body):
        def step(block, carry):
            body(block, chunk * blocks + block)
            return carry

        lax.fori_loop(0, blocks, step, 0)

    def attend(chunk):
        def make(block, carry):
            place = chunk * blocks + block
            rows_in = turned[place]
            query = (dot(joined_weight[0].reshape(width, width), rows_in) + wide_column(QUERY_BIAS)).astype(BF16)
            joined[place, 0] = query
            joined[place, 1] = dot(joined_weight[1].reshape(width, width), rows_in).astype(BF16)
            value = (dot(joined_weight[2].reshape(width, width), rows_in) + wide_column(VALUE_BIAS)).astype(BF16)
            joined[place, 2] = value
            scaled[block] = query * jnp.array(scale, BF16)
            key_codes[block] = jnp.broadcast_to(codes_ref[place].T[:, 1:2], (BLOCK, 128))
            turn_heads(1, key_rows, block, place)
            for head in range(heads):
                value_rows[head, block, :HEAD_DIM] = value[head * HEAD_DIM : (head + 1) * HEAD_DIM]
                value_rows[head, block, HEAD_DIM:] = jnp.ones((16, BLOCK), BF16)
            return carry

        lax.fori_loop(0, blocks, make, 0)

        def query_step(query_block, carry):
            here = chunk * blocks + query_block

            def score_step(key_block, highest):
                bias = block_bias(key_codes, codes_ref, here, key_block, query_block - key_block)
                fresh = []
                for head in range(heads):
                    rows_of = slice(head * HEAD_DIM, (head + 1) * HEAD_DIM)
                    score = dot(key_rows[head, key_block], scaled[query_block, rows_of, :]) + bias
                    first_sum[pl.ds(pl.multiple_of((head * blocks + key_block) * BLOCK, BLOCK), BLOCK), :] = score
                    fresh.append(
                        jnp.maximum(highest[head], jnp.max(score.reshape(BLOCK // 8, 8, BLOCK), axis=0))
                    )
                return tuple(fresh)

            low = jnp.full((8, BLOCK), 2 * NEGATIVE, F32)
            highest = lax.fori_loop(0, blocks, score_step, (low,) * heads)
            highest = [jnp.max(part, axis=0, keepdims=True) for part in highest]
            totals[...] = jnp.zeros_like(totals)

            def value_step(key_block, carry):
                for head in range(heads):
                    weights = jnp.exp(first_sum[pl.ds(pl.multiple_of((head * blocks + key_block) * BLOCK, BLOCK), BLOCK), :] - highest[head]).astype(BF16)
                    totals[head] += dot(value_rows[head, key_block], weights)
                return carry

            lax.fori_loop(0, blocks, value_step, 0)
            for head in range(heads):
                rows_of = slice(head * HEAD_DIM, (head + 1) * HEAD_DIM)
                whole = totals[head, HEAD_DIM : HEAD_DIM + 1, :]
                context[here, rows_of, :] = (totals[head, :HEAD_DIM, :] / whole).astype(BF16)
                logsums[here, head : head + 1, :] = highest[head] + jnp.log(whole)
            return carry

        lax.fori_loop(0, blocks, query_step, 0)
        begin("contexts", chunk)

    def attend_back(chunk):
        arrive("context_back", chunk)
        for kind in range(3):
            second_sum[kind * blocks : (kind + 1) * blocks] = jnp.zeros((blocks, width, BLOCK), F32)

        def make(block, carry):
            place = chunk * blocks + block
            scaled[block] = joined[place, 0] * jnp.array(scale, BF16)
            key_codes[block] = jnp.broadcast_to(codes_ref[place].T[:, 1:2], (BLOCK, 128))
            product = context_back[place].astype(F32) * context[place].astype(F32)
            turn_heads(1, key_rows, block, place)
            for head in range(heads):
                rows_of = slice(head * HEAD_DIM, (head + 1) * HEAD_DIM)
                value_turned[head, block] = joined[place, 2, rows_of, :].T
                deltas[block, head : head + 1, :] = jnp.sum(product[rows_of], axis=0, keepdims=True)
            return carry

        lax.fori_loop(0, blocks, make, 0)

        def pair_step(index, carry):
            query_block, key_block = index // blocks, lax.rem(index, blocks)
            query_place, key_place = chunk * blocks + query_block, chunk * blocks + key_block
            bias = block_bias(key_codes, codes_ref, query_place, key_block, query_block - key_block)
            for head in range(heads):
                rows_of = slice(head * HEAD_DIM, (head + 1) * HEAD_DIM)
                query = scaled[query_block, rows_of, :]
                upstream = context_back[query_place, rows_of, :]
                logsum = logsums[query_place, head : head + 1, :]
                delta = deltas[query_block, head : head + 1, :]
                weights = jnp.exp(dot(key_rows[head, key_block], query) + bias - logsum)
                weight_back = dot(value_turned[head, key_block], upstream)
                score_back = (weights * (weight_back - delta)).astype(BF16)
                second_sum[2 * blocks + key_block, rows_of, :] += dot_nt(upstream, weights.astype(BF16))
                second_sum[blocks + key_block, rows_of, :] += dot_nt(query, score_back)
                second_sum[query_block, rows_of, :] += dot(joined[key_place, 1, rows_of, :], score_back)
            return carry

        lax.fori_loop(0, blocks * blocks, pair_step, 0)

        def finish(block, carry):
            place = chunk * blocks + block
            query_low = (second_sum[block] * scale).astype(BF16)
            key_low = second_sum[blocks + block].astype(BF16)
            value_low = second_sum[2 * blocks + block].astype(BF16)
            rows_in = turned[place]
            joined_grad[0] += dot_nt(query_low, rows_in)
            joined_grad[1] += dot_nt(key_low, rows_in)
            joined_grad[2] += dot_nt(value_low, rows_in)
            sums[BIAS_EXPAND + (hidden.shape[0] // width)] += halves(query_low.astype(F32))
            sums[BIAS_EXPAND + (hidden.shape[0] // width) + 1] += halves(value_low.astype(F32))
            input_grad_ref[place] = (
                input_grad_ref[place]
                + dot(joined_turned[0], query_low)
                + dot(joined_turned[1], key_low)
                + dot(joined_turned[2], value_low)
            )
            return carry

        lax.fori_loop(0, blocks, finish, 0)

    zero = jnp.zeros((8, BLOCK), F32)

    def project(chunk):
        arrive("contexts", chunk)
        contexts[chunk, me] = context[chunk * blocks + me]
        attended = dot(output_turned[...], contexts[chunk].reshape(cols * width, BLOCK))
        for group in range(cols):
            spread_out[chunk, group] = attended[group * width : (group + 1) * width].astype(BF16)
        begin("attended", chunk)
        spread_in[chunk, me] = spread_out[chunk, me]

    def add_first(chunk):
        arrive("attended", chunk)

        def body(block, place):
            def part(at, carry):
                here = pl.ds(at, ROWS)
                summed = (
                    turned[place, here, :].astype(F32)
                    + spread_in[chunk, block, here, :].astype(F32)
                    + column(OUTPUT_BIAS, at)
                )
                first_sum[pl.ds(pl.multiple_of(place * width + at, ROWS), ROWS), :] = summed
                return carry[0] + fold(summed), carry[1] + fold(summed * summed)

            one, two = over_rows(width, part, (zero, zero))
            stat_out[chunk, pl.ds(2 * block, 1), :] = total(one)
            stat_out[chunk, pl.ds(2 * block + 1, 1), :] = total(two)

        over_blocks(chunk, body)
        begin("first", chunk)

    def gathered(own, others, chunk, index):
        summed = jnp.zeros((1, BLOCK), F32)
        for source in range(cols):
            summed += others[chunk, source, pl.ds(index, 1), :]
        return summed

    def feed_forward(chunk):
        arrive("first", chunk)
        stat_in[chunk, me] = stat_out[chunk]

        def body(block, place):
            center = gathered(stat_out, stat_in, chunk, 2 * block) / D
            inverse = lax.rsqrt(
                gathered(stat_out, stat_in, chunk, 2 * block + 1) / D - center * center + EPSILON
            )
            first_inverse[place] = inverse

            def normalize(at, carry):
                here = pl.ds(at, ROWS)
                normal = (first_sum[pl.ds(pl.multiple_of(place * width + at, ROWS), ROWS), :] - center) * inverse
                first_sum[pl.ds(pl.multiple_of(place * width + at, ROWS), ROWS), :] = normal
                middle_low[place, here, :] = (
                    normal * column(FIRST_GAIN, at) + column(FIRST_SHIFT, at)
                ).astype(BF16)
                return carry

            over_rows(width, normalize, 0)
            hidden[...] = dot(expand_turned[...], middle_low[place])
            for quarter in range(hidden.shape[0] // width):

                def gelu(at, carry):
                    here = pl.ds(quarter * width + at, ROWS)
                    value = hidden[here, :] + column(EXPAND_BIAS + quarter, at)
                    share = 0.5 * (1.0 + lax.erf(value * ROOT_HALF))
                    activated[place, here, :] = (value * share).astype(BF16)
                    slope[place, here, :] = (
                        share + value * DENSITY_SCALE * jnp.exp(-0.5 * value * value)
                    ).astype(BF16)
                    return carry

                over_rows(width, gelu, 0)
            narrow[...] = dot(reduce_turned[...], activated[place])

            def add_second(at, carry):
                here = pl.ds(at, ROWS)
                middle = first_sum[pl.ds(pl.multiple_of(place * width + at, ROWS), ROWS), :] * column(FIRST_GAIN, at) + column(FIRST_SHIFT, at)
                summed = middle + narrow[here, :] + column(REDUCE_BIAS, at)
                second_sum[place, here, :] = summed
                scaled = result_ref[place, here, :].astype(F32) * column(SECOND_GAIN, at)
                return (
                    carry[0] + fold(summed),
                    carry[1] + fold(summed * summed),
                    carry[2] + fold(scaled),
                    carry[3] + fold(scaled * summed),
                )

            found = over_rows(width, add_second, (zero,) * 4)
            for kind in range(4):
                wide_out[chunk, pl.ds(4 * block + kind, 1), :] = total(found[kind])

        over_blocks(chunk, body)
        begin("second", chunk)

    def feed_back(chunk):
        arrive("second", chunk)
        wide_in[chunk, me] = wide_out[chunk]

        def body(block, place):
            found = [gathered(wide_out, wide_in, chunk, 4 * block + kind) for kind in range(4)]
            center = found[0] / D
            inverse = lax.rsqrt(found[1] / D - center * center + EPSILON)
            mean_scaled = found[2] / D
            mean_product = inverse * (found[3] - center * found[2]) / D

            def back_norm(at, carry):
                here = pl.ds(at, ROWS)
                normal = (second_sum[place, here, :] - center) * inverse
                upstream = result_ref[place, here, :].astype(F32)
                gain = column(SECOND_GAIN, at)
                low_rows[here, :] = (normal * gain + column(SECOND_SHIFT, at)).astype(BF16)
                back = inverse * (upstream * gain - mean_scaled - normal * mean_product)
                second_sum[place, here, :] = back
                add_sum(GAIN_SECOND, at, upstream * normal)
                add_sum(SHIFT_SECOND, at, upstream)
                add_sum(BIAS_REDUCE, at, back)
                return carry

            over_rows(width, back_norm, 0)
            result_ref[place] = low_rows[...]
            back_low = second_sum[place].astype(BF16)
            hidden[...] = dot(reduce_natural[...], back_low)
            for quarter in range(hidden.shape[0] // width):

                def back_gelu(at, carry):
                    here = pl.ds(quarter * width + at, ROWS)
                    back = (hidden[here, :] * slope[place, here, :].astype(F32)).astype(BF16)
                    hidden_back[here, :] = back
                    add_sum(BIAS_EXPAND + quarter, at, back.astype(F32))
                    return carry

                over_rows(width, back_gelu, 0)
            grad_reduce[...] += dot_nt(back_low, activated[place])
            grad_expand[...] += dot_nt(hidden_back[...], middle_low[place])
            narrow[...] = dot(expand_natural[...], hidden_back[...])

            def add_middle(at, carry):
                here = pl.ds(at, ROWS)
                back = second_sum[place, here, :] + narrow[here, :]
                second_sum[place, here, :] = back
                normal = first_sum[pl.ds(pl.multiple_of(place * width + at, ROWS), ROWS), :]
                add_sum(GAIN_FIRST, at, back * normal)
                add_sum(SHIFT_FIRST, at, back)
                scaled = back * column(FIRST_GAIN, at)
                return carry[0] + fold(scaled), carry[1] + fold(scaled * normal)

            one, two = over_rows(width, add_middle, (zero, zero))
            back_out[chunk, pl.ds(2 * block, 1), :] = total(one)
            back_out[chunk, pl.ds(2 * block + 1, 1), :] = total(two)

        over_blocks(chunk, body)
        begin("third", chunk)

    def first_backward(chunk):
        arrive("third", chunk)
        back_in[chunk, me] = back_out[chunk]

        def body(block, place):
            mean_scaled = gathered(back_out, back_in, chunk, 2 * block) / D
            mean_product = gathered(back_out, back_in, chunk, 2 * block + 1) / D
            inverse = first_inverse[place]

            def part(at, carry):
                here = pl.ds(at, ROWS)
                back = inverse * (
                    second_sum[place, here, :] * column(FIRST_GAIN, at)
                    - mean_scaled
                    - first_sum[pl.ds(pl.multiple_of(place * width + at, ROWS), ROWS), :] * mean_product
                )
                input_grad_ref[place, here, :] = back
                middle_low[place, here, :] = back.astype(BF16)
                add_sum(BIAS_OUTPUT, at, back)
                return carry

            over_rows(width, part, 0)

        over_blocks(chunk, body)
        begin("backs", chunk)
        spread_in[chunk, me] = middle_low[chunk * blocks + me]

    def project_back(chunk):
        arrive("backs", chunk)
        for copy in transfers("attended", chunk):
            copy.wait_send()
        received = spread_in[chunk].reshape(cols * width, BLOCK)
        back = dot(output_natural[...], received)
        for group in range(cols):
            spread_out[chunk, group] = back[group * width : (group + 1) * width].astype(BF16)
        begin("context_back", chunk)
        context_back[chunk * blocks + me] = spread_out[chunk, me]
        every = contexts[chunk].reshape(cols * width, BLOCK)
        fresh = dot_nt(received, every)
        if chunk == 0:
            grad_output[...] = fresh
        else:
            grad_output[...] += fresh

    core, high = lax.rem(row, 2), row // 2
    sibling, opposite = row + 1 - 2 * core, lax.rem(row + 2, rows)
    there, side_here = 1 - high, high
    far, near = 2 * there + core, 2 * side_here + core
    portion = width // rows

    def portion_rows(owner):
        return pl.ds(pl.multiple_of(owner * portion, 8), portion)

    def piece(kind, owner):
        if kind == 0:
            return grad_output[pl.ds(pl.multiple_of(owner * width, 8), width), :]
        if kind == 1:
            return joined_grad[:, portion_rows(owner), :]
        if kind == 2:
            return grad_expand[pl.ds(pl.multiple_of(owner * width, 8), width), :]
        return grad_reduce[portion_rows(owner), :]

    one = (one_output, one_joined, one_expand, one_reduce, vectors_a)
    got = (got_output, got_joined, got_expand, got_reduce, got_vectors_a)
    two = (two_output, two_joined, two_expand, two_reduce, vectors_b)
    fars = (far_output, far_joined, far_expand, far_reduce, got_vectors_b)
    nears = (near_output, near_joined, near_expand, near_reduce, vectors_c)
    lasts = (last_output, last_joined, last_expand, last_reduce, vectors_c)
    alls = (all_output, all_joined, all_expand, all_reduce, got_vectors_c)

    def first_copy(kind):
        return remote(one[kind], got[kind], grad_send.at[0, kind], grad_recv.at[0, kind], "row", sibling)

    def second_copy(kind):
        return remote(two[kind], fars[kind], grad_send.at[1, kind], grad_recv.at[1, kind], "row", opposite)

    def col_copies():
        made = []
        for distance in range(1, cols):
            peer = peer_of("col", cols, distance)
            place = distance - 1
            made.append(remote(col_output.at[peer], col_got.at[me], col_send.at[place], col_recv.at[place], "col", peer))
        return made

    def last_copies(kind):
        made = []
        for distance in range(1, devices):
            peer = peer_of("dp", devices, distance)
            place = (kind, distance - 1)
            made.append(
                remote(lasts[kind], alls[kind].at[data], last_send.at[place], last_recv.at[place], "dp", peer)
            )
        return made

    def to_sibling(kinds_sent):
        for kind in kinds_sent:
            if kind == 4:
                vectors_a[...] = jnp.zeros_like(vectors_a)
                for index in range(sums.shape[0]):
                    vectors_a[index : index + 1, :] = jnp.sum(sums[index].T, axis=0, keepdims=True)
            else:
                for side in range(2):
                    one[kind][side] = piece(kind, 2 * side + 1 - core).astype(BF16)
            first_copy(kind).start()

    def to_opposite(kinds_sent):
        for kind in kinds_sent:
            first_copy(kind).wait_recv()
            if kind == 4:
                vectors_b[...] = vectors_a[...] + got_vectors_a[...]
            else:
                two[kind][...] = (piece(kind, far) + got[kind][there].astype(F32)).astype(BF16)
            second_copy(kind).start()
        for kind in kinds_sent:
            if kind != 4:
                nears[kind][...] = piece(kind, near) + got[kind][side_here].astype(F32)

    def to_data(kinds_sent):
        for kind in kinds_sent:
            second_copy(kind).wait_recv()
            if kind == 4:
                vectors_c[...] = vectors_b[...] + got_vectors_b[...]
            else:
                value = nears[kind][...] + fars[kind][...].astype(F32)
                nears[kind][...] = value
                lasts[kind][...] = value.astype(BF16)
            for copy in last_copies(kind):
                copy.start()

    def output_to_cols():
        second_copy(0).wait_recv()
        value = near_output[...] + far_output[...].astype(F32)
        for group in range(cols):
            own = value[:, group * width : (group + 1) * width]
            col_full[group] = own
            col_output[group] = own.astype(BF16)
        for copy in col_copies():
            copy.start()

    def output_to_data():
        for copy in col_copies():
            copy.wait_recv()
        value = col_full[me]
        for distance in range(1, cols):
            value += col_got[source_of("col", cols, distance)].astype(F32)
        col_full[me] = value
        last_output[...] = value.astype(BF16)
        for copy in last_copies(0):
            copy.start()

    def over_data(kind, value):
        for copy in last_copies(kind):
            copy.wait_recv()
        for distance in range(1, devices):
            value += alls[kind][source_of("dp", devices, distance)].astype(F32)
        return value

    for copy in joined_copies:
        copy.wait_recv()
    attend(0)
    for copy in output_copies:
        copy.wait_recv()
    for copy in row_copies:
        copy.start()
    output_parts[row] = output_columns[...]
    for kind in range(3):
        joined_turned[kind] = joined_weight[kind].reshape(width, width).T
    attend(1)
    for copy in row_copies:
        copy.wait_recv()
    for group in range(cols):
        here = slice(group * width, (group + 1) * width)
        output_natural[here, :] = jnp.concatenate([output_parts[part, group] for part in range(rows)], axis=1)
    for part in range(rows):
        here = slice(part * width, (part + 1) * width)
        output_turned[here, :] = jnp.concatenate(
            [output_parts[part, group].T for group in range(cols)], axis=1
        )
    project(0)
    attend(2)
    project(1)
    for copy in other_copies:
        copy.wait_recv()
    expand_natural[...] = jnp.concatenate([expand_parts[part] for part in range(rows)], axis=1)
    for part in range(rows):
        expand_turned[part * width : (part + 1) * width, :] = expand_parts[part].T
    reduce_turned[...] = reduce_parts[...].reshape(reduce_turned.shape)
    reduce_natural[...] = reduce_turned[...].T
    add_first(0)
    feed_forward(0)
    project(2)
    add_first(1)
    feed_back(0)
    feed_forward(1)
    first_backward(0)
    add_first(2)
    feed_back(1)
    feed_forward(2)
    first_backward(1)
    project_back(0)
    feed_back(2)
    project_back(1)
    first_backward(2)
    attend_back(0)
    project_back(2)
    to_sibling((0, 2, 3))
    attend_back(1)
    to_opposite((0, 2, 3))
    attend_back(2)
    to_sibling((1, 4))
    output_to_cols()
    to_data((2, 3))
    to_opposite((1, 4))
    output_to_data()
    to_data((1, 4))
    expand_out_ref[...] = over_data(2, near_expand[...]).T
    reduce_out_ref[...] = over_data(3, near_reduce[...])
    output_out_ref[...] = over_data(0, col_full[me]).T
    total_joined = over_data(1, near_joined[...])
    query_out_ref[...] = total_joined[0]
    key_out_ref[...] = total_joined[1]
    value_out_ref[...] = total_joined[2]
    vectors_out_ref[...] = over_data(4, vectors_c[...])
    for copy in joined_copies + output_copies + row_copies + other_copies + col_copies():
        copy.wait_send()
    for kind in kinds:
        for chunk in range(chunks):
            if kind != "attended":
                for copy in transfers(kind, chunk):
                    copy.wait_send()
    for kind in range(5):
        first_copy(kind).wait_send()
        second_copy(kind).wait_send()
        for copy in last_copies(kind):
            copy.wait_send()


def layer(devices, rows, cols, pairs, cotangent, codes, vectors, query, key, value, output, expand, reduce):
    width = output.shape[0]
    heads = width // HEAD_DIM
    every = pairs.shape[0] // PAIRS
    blocks = LEN // BLOCK
    chunks = every // blocks
    wide = expand.shape[1] * rows
    most = max(rows, cols) - 1
    part = width // rows
    count = 16
    kinds = BIAS_EXPAND + wide // width + 2

    def low(*shape):
        return pltpu.VMEM(shape, BF16)

    def full(*shape):
        return pltpu.VMEM(shape, F32)

    shapes = ((3, part, width), (width, cols * width), (width, width), (part, wide))
    dma = pltpu.SemaphoreType.DMA
    return pl.pallas_call(
        functools.partial(layer_kernel, devices, rows, cols),
        out_shape=(
            jax.ShapeDtypeStruct((every, width, BLOCK), BF16),
            jax.ShapeDtypeStruct((every, width, BLOCK), F32),
        ) + tuple(
            jax.ShapeDtypeStruct(shape, F32)
            for shape in ((part, width),) * 3 + ((width, width), (width, width), (part, wide), (count, width))
        ),
        in_specs=[vmem_spec()] * 10,
        out_specs=(vmem_spec(),) * 9,
        scratch_shapes=[
            low(every, width, BLOCK), low(every, 3, width, BLOCK), low(every, width, BLOCK), full(every, 8, BLOCK),
            full(blocks, BLOCK, 128), low(heads, blocks, BLOCK, HEAD_DIM), low(heads, blocks, HEAD_DIM + 16, BLOCK),
            low(heads, blocks, BLOCK, HEAD_DIM), low(blocks, width, BLOCK),
            full(heads, HEAD_DIM + 16, BLOCK), full(blocks, 8, BLOCK),
            low(3, rows, part, width), low(3, width, width), full(3, width, width),
            low(every, width, BLOCK),
            full(rows * width, cols * width), full(wide, width), full(width, wide), full(kinds, width, 128),
            low(chunks, cols, width, BLOCK), low(chunks, cols, width, BLOCK), low(chunks, cols, width, BLOCK),
            full(chunks, 2 * blocks, BLOCK), full(chunks, cols, 2 * blocks, BLOCK),
            full(chunks, 4 * blocks, BLOCK), full(chunks, cols, 4 * blocks, BLOCK),
            full(chunks, 2 * blocks, BLOCK), full(chunks, cols, 2 * blocks, BLOCK),
            low(cols, width, width), low(rows, cols, width, width), low(rows, width, width), low(rows, *reduce.shape),
            low(D, D), low(D, D), low(width, wide), low(wide, width), low(wide, width), low(width, wide),
            full(EXPAND_BIAS + wide // width, width, 128),
            full(max(every * width, heads * LEN), BLOCK), full(max(every, 3 * blocks), width, BLOCK),
            low(every, width, BLOCK), full(every, 1, BLOCK),
            full(wide, BLOCK), low(every, wide, BLOCK), low(every, wide, BLOCK),
            low(wide, BLOCK), full(width, BLOCK), low(width, BLOCK),
            *(low(2, *shape) for shape in shapes), full(count, width),
            *(low(2, *shape) for shape in shapes), full(count, width),
            *(low(*shape) for shape in shapes), full(count, width),
            *(low(*shape) for shape in shapes), full(count, width),
            *(full(*shape) for shape in shapes),
            low(cols, width, width), low(cols, width, width), full(cols, width, width),
            low(width, width), low(*shapes[0]), low(width, width), low(part, wide), full(count, width),
            low(devices, width, width), low(devices, *shapes[0]), low(devices, width, width),
            low(devices, part, wide), full(devices, count, width),
            dma((7, most)), dma((7, most)), dma((7, chunks, most)), dma((7, chunks, most)),
            dma((2, 5)), dma((2, 5)), dma((cols - 1,)), dma((cols - 1,)),
            dma((5, devices - 1)), dma((5, devices - 1)),
        ],
        compiler_params=pltpu.CompilerParams(
            collective_id=1, has_side_effects=True, vmem_limit_bytes=67043328
        ),
        name="layer",
    )(pairs, cotangent, codes, vectors, query, key, value, output, expand, reduce)


def finish_kernel(count, *refs):
    result_ref, grad_ref, vectors_ref = refs[:3]
    weights, outputs = refs[3:9], refs[9:]
    outputs[0][...] = pairs_of(result_ref[0])
    outputs[1][...] = pairs_of(grad_ref[0])

    @pl.when(pl.program_id(0) == 0)
    def once():
        for source, target in zip(weights, outputs[2:8]):
            target[...] = source[...]
        for kind in range(count):
            outputs[8 + kind][...] = vectors_ref[kind : kind + 1, :]


def finish_layer(result, grad, vectors, weights, count):
    every, width, unused = result.shape

    def whole(*shape):
        return pl.BlockSpec(shape, lambda i: (0,) * len(shape))

    block = pl.BlockSpec((1, width, BLOCK), lambda i: (i, 0, 0))
    pairs = pl.BlockSpec((PAIRS, 2 * width), lambda i: (i, 0))
    return pl.pallas_call(
        functools.partial(finish_kernel, count),
        out_shape=(
            jax.ShapeDtypeStruct((every * PAIRS, 2 * width), BF16),
            jax.ShapeDtypeStruct((every * PAIRS, 2 * width), F32),
            *(jax.ShapeDtypeStruct(weight.shape, F32) for weight in weights),
            *(jax.ShapeDtypeStruct((1, width), F32) for kind in range(count)),
        ),
        grid=(every,),
        in_specs=[block, block, whole(*vectors.shape)] + [whole(*weight.shape) for weight in weights],
        out_specs=(
            pairs, pairs, *(whole(*weight.shape) for weight in weights), *(whole(1, width) for kind in range(count)),
        ),
        name="finish_layer",
    )(result, grad, vectors, *weights)


def local(
    devices, rows, cols,
    inputs, segment_ids, keep_mask, query_weight, query_bias, key_weight, value_weight, value_bias,
    output_weight, output_bias, first_gain, first_shift, expand_weight, expand_bias, reduce_weight,
    reduce_bias, second_gain, second_shift, cotangent,
):
    width = query_bias.shape[0]
    every = segment_ids.shape[0] // BLOCK
    coded = jnp.stack([segment_ids, jnp.where(keep_mask == 1, segment_ids, -1)]).astype(F32)
    coded = coded.reshape(2, every, PAIRS, 2).transpose(1, 0, 3, 2).reshape(every, 2, BLOCK)
    codes = jnp.pad(coded, ((0, 0), (0, 6), (0, 0)))
    stacked = [
        query_bias, value_bias, output_bias, first_gain, first_shift, reduce_bias, second_gain, second_shift,
    ]
    vectors = jnp.concatenate([jnp.stack(stacked), expand_bias.reshape(-1, width)])
    vectors = jnp.pad(vectors, ((0, -vectors.shape[0] % 8), (0, 0)))
    result, grad, query, key, value, output, expand, reduce, found = layer(
        devices, rows, cols, inputs[:, 0, :], cotangent[:, 0, :], codes, vectors,
        query_weight.T, key_weight.T, value_weight.T, output_weight, expand_weight, reduce_weight.T,
    )
    quarters = expand_bias.shape[0] // width
    count = BIAS_EXPAND + quarters + 2
    finished = finish_layer(result, grad, found, (query, key, value, output, expand, reduce), count)
    result, grad, query, key, value, output, expand, reduce = finished[:8]
    found = [part[0] for part in finished[8:]]
    last = BIAS_EXPAND + quarters
    return (
        result[:, None, :], grad[:, None, :],
        query.T, found[last], key.T, value.T, found[last + 1], output, found[BIAS_OUTPUT],
        found[GAIN_FIRST], found[SHIFT_FIRST], expand, jnp.concatenate(found[BIAS_EXPAND:last]), reduce.T,
        found[BIAS_REDUCE], found[GAIN_SECOND], found[SHIFT_SECOND],
    )


def solution(mesh):
    tokens, weight, vector = P(("dp", "row"), "col", None), P("col", "row"), P("col")
    ids = P(("dp", "row"))
    return jax.shard_map(
        functools.partial(local, mesh.shape["dp"], mesh.shape["row"], mesh.shape["col"]),
        mesh=mesh,
        in_specs=(
            tokens, ids, ids, weight, vector, weight, weight, vector, weight, vector, vector, vector, weight,
            vector, weight, vector, vector, vector, tokens,
        ),
        out_specs=(
            tokens, tokens, weight, vector, weight, weight, vector, weight, vector, vector, vector, weight,
            vector, weight, vector, vector, vector,
        ),
        check_vma=False,
    )
```

time: 285 us -> 229 us (0.80); the launches traced: 280 us -> 228 us
  Pallas kernels: 261 us -> 215 us
  local copies, waits for them, and re-layouts: 17.7 us -> 11.4 us
    pallas_call x5 -> x2, Pallas kernels: 261 us -> 215 us  [the longest x1 205 us: layer(): pl.pallas_call(functools.partial(layer_kernel, devices, rows, cols), out_...]
    unnamed x26 -> x11, local copies, waits for them, and re-layouts: 11.5 us -> 6.5 us
where the time goes in v3:
time: 229 us; the launch traced here: 228 us
  Pallas kernels  215 us (94%)
  local copies, waits for them, and re-layouts  11.4 us (5%)
    pallas_call x1, Pallas kernels, layer(): pl.pallas_call(functools.partial(layer_kernel, devices, rows, cols), out_...  205 us
    pallas_call x1, Pallas kernels, finish_layer(): pl.pallas_call(functools.partial(finish_kernel, count), out_shape=(jax.Sh...  9.57 us
    unnamed x11, local copies, waits for them, and re-layouts  6.5 us

profile of v3, /device:TPU:0, one launch (start us, length us, event | category | flops | bytes accessed | tf_op | source)
XLA Modules:
  0.0 228.2 jit_solution(10726759239197353076)
XLA Ops:
  0.7 0.0 copy-start
  0.7 0.8 reshape.46
  1.4 0.8 concatenate.7
  2.3 0.6 pad.9.vectors_ref
  2.9 0.7 compare_select_fusion
  3.6 0.7 stack.34
  4.3 0.3 copy.40
  4.6 0.0 copy-done
  4.6 0.7 stack.33
  5.4 0.3 copy.39
  5.7 0.7 pad.8.codes_ref
  6.4 205.0 %layer.1 = (bf16[12,192,256]{2,1,0:T(8,128)(2,1)}, f32[12,192,256]{2,1,0:T(8,128)}, f32[48,192]{1,0:T(8,128)}, f32[48,192]{1,0:T(8,128)}, f32[48,192]{1,0:T(8,12...) custom-call(bf16[1536,384]{1,0:T(8,128)(2,1)} %bitcast.35, ...), custom_call_target="tpu_custom_call" | custom-call | tf_op jit(solution)/shard_map/layer/pallas_call | solution.py:768
  211.4 9.6 %finish_layer.1 = (bf16[1536,384]{1,0:T(8,128)(2,1)}, f32[1536,384]{1,0:T(8,128)}, f32[48,192]{1,0:T(8,128)}, f32[48,192]{1,0:T(8,128)}, f32[48,192]{1,0:T(8,128...) custom-call(bf16[12,192,256]{2,1,0:T(8,128)(2,1)} %get-tuple-element, ...), custom_call_target="tpu_custom_call" | custom-call | tf_op jit(solution)/shard_map/finish_layer/pallas_call | solution.py:840
  220.9 0.0 copy-start.1
  221.0 0.0 copy-start.2
  221.0 0.0 copy-start.3
  221.0 0.0 copy-start.4
  221.0 6.5 %copy.42 = f32[1536,1,384]{2,1,0:T(1,128)} copy(f32[1536,1,384]{2,0,1:T(8,128)} %bitcast.34) | data formatting | bytes 4718592
  227.5 0.0 copy-done.1
  227.5 0.0 copy-done.2
  227.5 0.0 copy-done.3
  227.5 0.0 copy-done.4
  227.5 0.7 pad_maximum_fusion
  (3 shorter events, 0.1 us)
Async XLA Ops:
  0.7 4.0 %copy-start = (s32[3072]{0:T(1024)S(1)}, s32[3072]{0:T(1024)}, u32[]{:S(2)}) copy-start(s32[3072]{0:T(1024)} %param.20) | copy-start | bytes 36868
  220.9 6.5 %copy-start.1 = (f32[1,192]{1,0:T(1,128)S(1)}, f32[1,192]{1,0:T(1,128)}, u32[]{:S(2)}) copy-start(f32[1,192]{1,0:T(1,128)} %get-tuple-element.67) | copy-start | bytes 2308
  221.0 6.5 %copy-start.2 = (f32[1,192]{1,0:T(1,128)S(1)}, f32[1,192]{1,0:T(1,128)}, u32[]{:S(2)}) copy-start(f32[1,192]{1,0:T(1,128)} %get-tuple-element.68) | copy-start | bytes 2308
  221.0 6.5 %copy-start.3 = (f32[1,192]{1,0:T(1,128)S(1)}, f32[1,192]{1,0:T(1,128)}, u32[]{:S(2)}) copy-start(f32[1,192]{1,0:T(1,128)} %get-tuple-element.69) | copy-start | bytes 2308
  221.0 6.5 %copy-start.4 = (f32[1,192]{1,0:T(1,128)S(1)}, f32[1,192]{1,0:T(1,128)}, u32[]{:S(2)}) copy-start(f32[1,192]{1,0:T(1,128)} %get-tuple-element.70) | copy-start | bytes 2308
